TPU v7x, 32 devices: a whole 2x2x4 slice. The times are simulated.
32 devices in a mesh: section: 4 (over y, x), fsdp: 8 (over z, core).
Axes of the slice: x: 2, y: 2, z: 4, core: 2. Of those that a mesh axis runs over, the one named last changes fastest.
Arguments:
- patches: bfloat16 [8, 1024, 768], P(None, 'fsdp'), may hold values from -6 to 6
- cotangent: bfloat16 [8, 1024, 768], P(None, 'fsdp'), may hold values from -6 to 6
- embed_blocks: int32 [8], replicated, may hold values from 4 to 6
- ratio_index: int32 [8], replicated, may hold values from 0 to 2
- depth: int32 [8], replicated, may hold values from 2 to 4
- w_up: bfloat16 [4, 768, 3072], P('section', 'fsdp'), may hold values from -0.21875 to 0.21875
- w_down: bfloat16 [4, 3072, 768], P('section', 'fsdp'), may hold values from -0.109375 to 0.109375
- ln_gain: bfloat16 [4, 768], P('section', 'fsdp'), may hold values from 0.099609375 to 1.8984375
Outputs:
- grad_up: float32 [4, 768, 3072], P('section', 'fsdp')
- grad_down: float32 [4, 3072, 768], P('section', 'fsdp')
- grad_gain: float32 [4, 768], P('section', 'fsdp')
All inputs are finite; a program needn't handle non-finite values.
Results may differ from a plain program's by a relative error of at most 0.028.
Values may be sent and summed in bfloat16 or wider, within the bound.
A program may use at most 192 MiB of HBM per device.

v0:
```python
import jax
import jax.numpy as jnp
from jax import lax
from jax.sharding import PartitionSpec as P

BLOCK = 128


EPSILON = 1e-05


def passed_along(block, axis, distance):
    devices = range(lax.axis_size(axis))
    route = [(i - distance, i) for i in devices if i - distance in devices]
    return lax.ppermute(block, axis, route)


def micro_masks(blocks, ratio, feature_count, hidden_count):
    width_int = blocks * BLOCK
    hidden_int = width_int * (6 + ratio) // 2
    embed_mask = (lax.iota(jnp.int32, feature_count) < width_int).astype(jnp.float32)
    hidden_mask = (lax.iota(jnp.int32, hidden_count) < hidden_int).astype(jnp.float32)
    return (embed_mask, hidden_mask, width_int.astype(jnp.float32))


def layer_norm(inputs, embed_mask, width_float):
    values = inputs.astype(jnp.float32) * embed_mask
    center_value = jnp.sum(values, axis=-1, keepdims=True) / width_float
    centered = (values - center_value) * embed_mask
    variance = jnp.sum(centered * centered, axis=-1, keepdims=True) / width_float
    inv_std = lax.rsqrt(variance + EPSILON)
    return (centered * inv_std, inv_std)


def run_ticks(total, tick, carry):
    for number in range(total):
        carry = tick(number, carry)
    return carry


def gelu_and_slope(hidden):
    square = hidden * hidden
    scale = 0.7978845608028654
    tanh = jnp.tanh(scale * hidden * (1.0 + 0.044715 * square))
    half = 0.5 * (1.0 + tanh)
    slope = half + (0.5 * scale) * hidden * (1.0 - tanh * tanh) * (1.0 + 0.134145 * square)
    return (hidden * half, slope)


def contract_rows(left, right):
    return lax.dot_general(
        left, right, (((0,), (0,)), ((), ())), preferred_element_type=jnp.float32
    )


def contract_last(left, right):
    return lax.dot_general(
        left, right, (((1,), (1,)), ((), ())), preferred_element_type=jnp.float32
    )


def store_row(stash, value, slot):
    return lax.dynamic_update_index_in_dim(stash, value, slot, 0)


HOP_TICKS = 2
EXTRA_ROWS = 16


def per_device(patches, cotangent, embed_blocks, ratio_index, depth, w_up, w_down, ln_gain):
    section_count = lax.axis_size("section")
    section_index = lax.axis_index("section")
    shard_count = lax.axis_size("fsdp")
    micro_count, row_count, feature_count = patches.shape
    hidden_count = w_up.shape[2]
    down_rows = w_down.shape[1]
    gain_count = ln_gain.shape[1]
    tick_total = micro_count + HOP_TICKS * (section_count - 1)
    bf16 = jnp.bfloat16

    gain_rows = jnp.pad(ln_gain, ((0, EXTRA_ROWS - 1), (0, feature_count - gain_count)))
    packed_down = jnp.concatenate([w_down[0], gain_rows], axis=0)
    weight_up = lax.all_gather(w_up[0], "fsdp", axis=0, tiled=True)
    gathered_down = lax.all_gather(packed_down, "fsdp", axis=0, tiled=True)
    gathered_down = gathered_down.reshape(shard_count, down_rows + EXTRA_ROWS, feature_count)
    weight_down = gathered_down[:, :down_rows].reshape(hidden_count, feature_count)
    gain = gathered_down[:, down_rows, :gain_count].reshape(feature_count).astype(jnp.float32)

    def masks_of(micro_index):
        is_valid = jnp.logical_and(micro_index >= 0, micro_index < micro_count)
        safe_index = jnp.clip(micro_index, 0, micro_count - 1)
        slot = jnp.where(is_valid, micro_index, micro_count)
        embed_mask, hidden_mask, width_float = micro_masks(
            embed_blocks[safe_index], ratio_index[safe_index], feature_count, hidden_count
        )
        active = (section_index < depth[safe_index]).astype(jnp.float32)
        return (safe_index, slot, is_valid, embed_mask, hidden_mask, active, width_float)

    def forward_tick(tick, carry):
        previous, incoming, stash_in, stash_act, stash_slope = carry
        sent = passed_along(previous, "section", 1)
        safe, slot, is_valid, embed_mask, hidden_mask, active, width = masks_of(
            tick - HOP_TICKS * section_index
        )
        first_in = (patches[safe].astype(jnp.float32) * embed_mask).astype(bf16)
        inputs = jnp.where(section_index == 0, first_in, incoming)
        standard, inv_std = layer_norm(inputs, embed_mask, width)
        normed = (standard * gain).astype(bf16)
        hidden = jnp.dot(normed, weight_up, preferred_element_type=jnp.float32)
        value, slope = gelu_and_slope(hidden)
        act = (value * hidden_mask).astype(bf16)
        slope = (slope * hidden_mask).astype(bf16)
        branch = jnp.dot(act, weight_down, preferred_element_type=jnp.float32)
        output = (inputs.astype(jnp.float32) + active * embed_mask * branch).astype(bf16)
        return (
            output,
            sent,
            store_row(stash_in, inputs, slot),
            store_row(stash_act, act, slot),
            store_row(stash_slope, slope, slot),
        )

    def empty(width):
        return jnp.zeros((micro_count + 1, row_count, width), bf16)

    nothing = jnp.zeros((row_count, feature_count), bf16)
    carry = (nothing, nothing, empty(feature_count), empty(hidden_count), empty(hidden_count))
    carry = run_ticks(tick_total, forward_tick, carry)
    unused_out, unused_sent, stash_in, stash_act, stash_slope = carry

    def backward_tick(tick, carry):
        previous, incoming, acc_gain, stash_branch, stash_hidden, stash_normed = carry
        sent = passed_along(previous, "section", -1)
        safe, slot, is_valid, embed_mask, hidden_mask, active, width = masks_of(
            tick - HOP_TICKS * (section_count - 1 - section_index)
        )
        last_in = (cotangent[safe].astype(jnp.float32) * embed_mask).astype(bf16)
        grad_out = jnp.where(section_index == section_count - 1, last_in, incoming)
        grad_float = grad_out.astype(jnp.float32)
        live = jnp.where(is_valid, active, 0.0)
        grad_branch = (live * embed_mask * grad_float).astype(bf16)
        grad_act = contract_last(grad_branch, weight_down)
        grad_hidden = (grad_act * stash_slope[slot].astype(jnp.float32)).astype(bf16)
        grad_normed = contract_last(grad_hidden, weight_up)
        standard, inv_std = layer_norm(stash_in[slot], embed_mask, width)
        normed = (standard * gain).astype(bf16)
        grad_standard = grad_normed * gain * embed_mask
        acc_gain = acc_gain + jnp.sum(grad_normed * standard, axis=0)
        first_mean = jnp.sum(grad_standard, axis=-1, keepdims=True) / width
        second_mean = jnp.sum(grad_standard * standard, axis=-1, keepdims=True) / width
        grad_norm_in = inv_std * (grad_standard - first_mean * embed_mask - standard * second_mean)
        grad_in = (grad_float + grad_norm_in).astype(bf16)
        return (
            grad_in,
            sent,
            acc_gain,
            store_row(stash_branch, grad_branch, slot),
            store_row(stash_hidden, grad_hidden, slot),
            store_row(stash_normed, normed, slot),
        )

    carry = (
        nothing,
        nothing,
        jnp.zeros((feature_count,), jnp.float32),
        empty(feature_count),
        empty(hidden_count),
        empty(feature_count),
    )
    carry = run_ticks(tick_total, backward_tick, carry)
    unused_out, unused_sent, acc_gain, stash_branch, stash_hidden, stash_normed = carry

    def flat(stash):
        return stash.reshape(-1, stash.shape[-1])

    part_down = contract_rows(flat(stash_act), flat(stash_branch)).astype(bf16)
    part_gain = acc_gain.astype(bf16).reshape(shard_count, 1, gain_count)
    part_gain = jnp.pad(
        part_gain, ((0, 0), (0, EXTRA_ROWS - 1), (0, feature_count - gain_count))
    )
    packed = jnp.concatenate(
        [part_down.reshape(shard_count, down_rows, feature_count), part_gain], axis=1
    ).reshape(-1, feature_count)
    own_down = lax.psum_scatter(packed, "fsdp", scatter_dimension=0, tiled=True)
    part_up = contract_rows(flat(stash_normed), flat(stash_hidden)).astype(bf16)
    own_up = lax.psum_scatter(part_up, "fsdp", scatter_dimension=0, tiled=True)
    grad_up = own_up.astype(jnp.float32)[None]
    grad_down = own_down[:down_rows].astype(jnp.float32)[None]
    grad_gain = own_down[down_rows, :gain_count].astype(jnp.float32)[None]
    return (grad_up, grad_down, grad_gain)


def solution(mesh):
    return jax.shard_map(
        per_device,
        mesh=mesh,
        in_specs=(
            P(None, "fsdp", None),
            P(None, "fsdp", None),
            P(),
            P(),
            P(),
            P("section", "fsdp", None),
            P("section", "fsdp", None),
            P("section", "fsdp"),
        ),
        out_specs=(P("section", "fsdp", None), P("section", "fsdp", None), P("section", "fsdp")),
        check_vma=False,
    )
```

profile of v0, /device:TPU:0, one launch (start us, length us, event | category | flops | bytes accessed | tf_op | source)
XLA Modules:
  0.0 531.3 jit_solution(3041586789958740881)
XLA Ops:
  7.2 2.0 fusion.109
  11.3 6.2 %collective-permute-start = (bf16[128,768]{1,0:T(8,128)(2,1)}, bf16[128,768]{1,0:T(8,128)(2,1)}, u32[]{:S(2)}, u32[]{:S(2)}) collective-permute-start(bf16[128,768]{1,0:T(8,128)(2,1)} %broadcast_in_dim.237), channel_id=1, source_target_pairs={{0,8},{8,16},{16,24},{1,9},{9,17},{17,25},{2,10},{10,18},{18,26},{... | collective-permute-start | bytes 589832 | tf_op jit(solution)/shard_map/ppermute | solution.py:15
  107.6 4.8 slice.17
  114.6 3.0 all-gather.6.cloned.1.call-done
  120.5 2.5 bitcast_dynamic-update-slice_fusion.13
  123.8 2.5 bitcast_dynamic-update-slice_fusion.41
  127.6 3.4 collective-permute-start.1
  131.0 1.9 bitcast_dynamic-update-slice_fusion.12
  134.1 3.6 collective-permute-start.2
  138.1 3.6 collective-permute-done.2
  142.2 1.9 bitcast_dynamic-update-slice_fusion.11
  145.3 4.4 collective-permute-start.3
  149.7 1.9 bitcast_dynamic-update-slice_fusion.10
  152.8 4.3 collective-permute-start.4
  157.5 2.7 collective-permute-done.4
  160.7 1.9 bitcast_dynamic-update-slice_fusion.9
  163.8 4.8 collective-permute-start.5
  168.6 1.9 bitcast_dynamic-update-slice_fusion.8
  171.7 3.0 collective-permute-start.6
  175.2 2.7 collective-permute-done.6
  178.4 1.9 bitcast_dynamic-update-slice_fusion.7
  181.5 4.4 collective-permute-start.7
  185.9 1.9 bitcast_dynamic-update-slice_fusion.6
  189.0 3.0 collective-permute-start.8
  192.4 2.5 collective-permute-done.8
  195.4 1.9 bitcast_dynamic-update-slice_fusion.5
  198.5 4.4 collective-permute-start.9
  202.9 1.9 bitcast_dynamic-update-slice_fusion.4
  206.1 2.8 collective-permute-start.10
  209.3 2.7 collective-permute-done.10
  212.5 1.9 bitcast_dynamic-update-slice_fusion.3
  215.5 4.6 collective-permute-start.11
  220.2 1.9 bitcast_dynamic-update-slice_fusion.2
  223.3 2.8 collective-permute-start.12
  226.6 2.7 collective-permute-done.12
  234.0 4.2 broadcast.1352
  238.9 2.5 bitcast_dynamic-update-slice_fusion.27
  241.5 2.5 bitcast_dynamic-update-slice_fusion.26
  244.0 1.9 fusion.248
  249.8 4.6 collective-permute-done.15
  256.1 1.9 fusion.286
  260.1 7.1 %collective-permute-done.17 = bf16[128,768]{1,0:T(8,128)(2,1)S(1)} collective-permute-done((bf16[128,768]{1,0:T(8,128)(2,1)S(1)}, bf16[128,768]{1,0:T(8,128)(2,1)S(1)}, u32[]{:S(2)}, u32[]{:S(2)}) %collective-permute-start.17) | collective-permute-done | bytes 196640 | tf_op jit(solution)/shard_map/ppermute | solution.py:15
  272.6 7.1 %collective-permute-done.19 = bf16[128,768]{1,0:T(8,128)(2,1)S(1)} collective-permute-done((bf16[128,768]{1,0:T(8,128)(2,1)S(1)}, bf16[128,768]{1,0:T(8,128)(2,1)S(1)}, u32[]{:S(2)}, u32[]{:S(2)}) %collective-permute-start.19) | collective-permute-done | bytes 196640 | tf_op jit(solution)/shard_map/ppermute | solution.py:15
  284.9 7.1 %collective-permute-done.21 = bf16[128,768]{1,0:T(8,128)(2,1)S(1)} collective-permute-done((bf16[128,768]{1,0:T(8,128)(2,1)S(1)}, bf16[128,768]{1,0:T(8,128)(2,1)S(1)}, u32[]{:S(2)}, u32[]{:S(2)}) %collective-permute-start.21) | collective-permute-done | bytes 196640 | tf_op jit(solution)/shard_map/ppermute | solution.py:15
  297.4 7.7 %collective-permute-done.23 = bf16[128,768]{1,0:T(8,128)(2,1)S(1)} collective-permute-done((bf16[128,768]{1,0:T(8,128)(2,1)S(1)}, bf16[128,768]{1,0:T(8,128)(2,1)S(1)}, u32[]{:S(2)}, u32[]{:S(2)}) %collective-permute-start.23) | collective-permute-done | bytes 196640 | tf_op jit(solution)/shard_map/ppermute | solution.py:15
  310.3 7.1 %collective-permute-done.14 = bf16[128,768]{1,0:T(8,128)(2,1)S(1)} collective-permute-done((bf16[128,768]{1,0:T(8,128)(2,1)S(1)}, bf16[128,768]{1,0:T(8,128)(2,1)S(1)}, u32[]{:S(2)}, u32[]{:S(2)}) %collective-permute-start.14) | collective-permute-done | bytes 196640 | tf_op jit(solution)/shard_map/ppermute | solution.py:15
  321.4 2.0 fusion.267
  326.5 8.8 %collective-permute-done.16 = bf16[128,768]{1,0:T(8,128)(2,1)S(1)} collective-permute-done((bf16[128,768]{1,0:T(8,128)(2,1)S(1)}, bf16[128,768]{1,0:T(8,128)(2,1)S(1)}, u32[]{:S(2)}, u32[]{:S(2)}) %collective-permute-start.16) | collective-permute-done | bytes 196640 | tf_op jit(solution)/shard_map/ppermute | solution.py:15
  338.8 2.0 fusion.305
  342.6 9.3 %collective-permute-done.18 = bf16[128,768]{1,0:T(8,128)(2,1)S(1)} collective-permute-done((bf16[128,768]{1,0:T(8,128)(2,1)S(1)}, bf16[128,768]{1,0:T(8,128)(2,1)S(1)}, u32[]{:S(2)}, u32[]{:S(2)}) %collective-permute-start.18) | collective-permute-done | bytes 196640 | tf_op jit(solution)/shard_map/ppermute | solution.py:15
  358.8 8.0 %collective-permute-done.20 = bf16[128,768]{1,0:T(8,128)(2,1)S(1)} collective-permute-done((bf16[128,768]{1,0:T(8,128)(2,1)S(1)}, bf16[128,768]{1,0:T(8,128)(2,1)S(1)}, u32[]{:S(2)}, u32[]{:S(2)}) %collective-permute-start.20) | collective-permute-done | bytes 196640 | tf_op jit(solution)/shard_map/ppermute | solution.py:15
  373.7 6.9 %collective-permute-done.22 = bf16[128,768]{1,0:T(8,128)(2,1)S(1)} collective-permute-done((bf16[128,768]{1,0:T(8,128)(2,1)S(1)}, bf16[128,768]{1,0:T(8,128)(2,1)S(1)}, u32[]{:S(2)}, u32[]{:S(2)}) %collective-permute-start.22) | collective-permute-done | bytes 196640 | tf_op jit(solution)/shard_map/ppermute | solution.py:15
  387.8 6.6 %collective-permute-done.24 = bf16[128,768]{1,0:T(8,128)(2,1)S(1)} collective-permute-done((bf16[128,768]{1,0:T(8,128)(2,1)S(1)}, bf16[128,768]{1,0:T(8,128)(2,1)S(1)}, u32[]{:S(2)}, u32[]{:S(2)}) %collective-permute-start.24) | collective-permute-done | bytes 196640 | tf_op jit(solution)/shard_map/ppermute | solution.py:15
  394.3 2.5 bitcast_dynamic-update-slice_fusion.15
  397.8 2.5 bitcast_dynamic-update-slice_fusion.14
  401.2 8.0 %bitcast_convert_fusion.1 = bf16[768,3072]{1,0:T(8,128)(2,1)} fusion(bf16[9,128,768]{2,1,0:T(8,128)(2,1)S(1)} %get-tuple-element.135, bf16[9,128,3072]{2,1,0:T(8,128)(2,1)S(1)} %get-tuple-element.251), kind=kOutput, calls=%fused_computation.3 | convolution fusion | flops 5438177280 | bytes 13565952 | tf_op jit(solution)/shard_map/dot_general | solution.py:51
  410.3 4.1 fusion.106
  414.4 4.1 fusion.103
  418.7 9.2 %bitcast_convert_fusion = bf16[3072,768]{1,0:T(8,128)(2,1)S(1)} fusion(bf16[9,128,3072]{2,1,0:T(8,128)(2,1)} %copy-done.2, bf16[9,128,768]{2,1,0:T(8,128)(2,1)} %get-tuple-element.134), kind=kOutput, calls=%fused_computation.2 | convolution fusion | flops 5438177280 | bytes 13565952 | tf_op jit(solution)/shard_map/dot_general | solution.py:51
  427.9 2.5 fusion.1
  430.4 33.2 %reduce-scatter.3.cloned.1.call-done = bf16[96,3072]{1,0:T(8,128)(2,1)} async-done(((bf16[768,3072]{1,0:T(8,128)(2,1)}), bf16[96,3072]{1,0:T(8,128)(2,1)}) %reduce-scatter.3.cloned.1.call-update) | async-done | bytes 589840 | tf_op jit(solution)/shard_map/reduce_scatter | solution.py:186
  463.6 2.2 bitcast_convert_fusion.2
  465.8 55.2 %reduce-scatter.5.cloned.1.call-done = bf16[400,768]{1,0:T(8,128)(2,1)} async-done(((bf16[3200,768]{1,0:T(8,128)(2,1)}), bf16[400,768]{1,0:T(8,128)(2,1)}) %reduce-scatter.5.cloned.1.call-update) | async-done | bytes 614416 | tf_op jit(solution)/shard_map/reduce_scatter | solution.py:184
  522.2 2.2 fusion.110
  (492 shorter events, 143.6 us)
Async XLA Ops:
  7.2 10.6 %copy-start.8 = (s32[8]{0:T(128)S(1)}, s32[8]{0:T(128)}, u32[]{:S(2)}) copy-start(s32[8]{0:T(128)} %param.10) | copy-start | bytes 100
  7.2 100.5 %all-gather.4.cloned.1.call-start = ((), (), s32[]{:S(2)}) async-start(), calls=%async_computation.2 | async-start | bytes 5529600 | tf_op jit(solution)/shard_map/all_gather | solution.py:84
  7.2 22.6 %copy-start.9 = (s32[8]{0:T(128)S(1)}, s32[8]{0:T(128)}, u32[]{:S(2)}) copy-start(s32[8]{0:T(128)} %param.12) | copy-start | bytes 100
  7.2 24.0 %copy-start.16 = (s32[8]{0:T(128)S(1)}, s32[8]{0:T(128)}, u32[]{:S(2)}) copy-start(s32[8]{0:T(128)} %param.11) | copy-start | bytes 100
  9.2 108.4 %all-gather.6.cloned.1.call-start = ((), (), s32[]{:S(2)}) async-start(), calls=%async_computation.5 | async-start | bytes 5308416 | tf_op jit(solution)/shard_map/all_gather | solution.py:83
  10.0 95.9 %collective-permute-start.13 = (bf16[128,768]{1,0:T(8,128)(2,1)}, bf16[128,768]{1,0:T(8,128)(2,1)}, u32[]{:S(2)}, u32[]{:S(2)}) collective-permute-start(bf16[128,768]{1,0:T(8,128)(2,1)} %broadcast_in_dim.237), channel_id=1, source_target_pairs={{8,0},{16,8},{24,16},{9,1},{17,9},{25,17},{10,2},{18,10},{26,18},{... | collective-permute-start | bytes 589832 | tf_op jit(solution)/shard_map/ppermute | solution.py:15
  11.3 92.7 %collective-permute-start = (bf16[128,768]{1,0:T(8,128)(2,1)}, bf16[128,768]{1,0:T(8,128)(2,1)}, u32[]{:S(2)}, u32[]{:S(2)}) collective-permute-start(bf16[128,768]{1,0:T(8,128)(2,1)} %broadcast_in_dim.237), channel_id=1, source_target_pairs={{0,8},{8,16},{16,24},{1,9},{9,17},{17,25},{2,10},{10,18},{18,26},{... | collective-permute-start | bytes 589832 | tf_op jit(solution)/shard_map/ppermute | solution.py:15
  17.5 446.1 %reduce-scatter.3.cloned.1.call-start = ((), (), s32[]{:S(2)}) async-start(), calls=%async_computation.3 | async-start | bytes 5308416 | tf_op jit(solution)/shard_map/reduce_scatter | solution.py:186
  72.8 32.3 %copy-start.35 = (f32[768]{0:T(1024)}, f32[768]{0:T(1024)S(1)}, u32[]{:S(2)}) copy-start(f32[768]{0:T(1024)S(1)} %fusion.721) | copy-start | bytes 9220
  72.8 29.9 %copy-start.37 = (f32[768]{0:T(1024)}, f32[768]{0:T(1024)S(1)}, u32[]{:S(2)}) copy-start(f32[768]{0:T(1024)S(1)} %fusion.723) | copy-start | bytes 9220
  79.3 26.6 %copy-start.47 = (f32[768]{0:T(1024)}, f32[768]{0:T(1024)S(1)}, u32[]{:S(2)}) copy-start(f32[768]{0:T(1024)S(1)} %fusion.696) | copy-start | bytes 9220
  79.3 23.3 %copy-start.49 = (f32[768]{0:T(1024)}, f32[768]{0:T(1024)S(1)}, u32[]{:S(2)}) copy-start(f32[768]{0:T(1024)S(1)} %fusion.698) | copy-start | bytes 9220
  89.4 13.3 %copy-start.14 = (f32[768]{0:T(1024)}, f32[768]{0:T(1024)S(1)}, u32[]{:S(2)}) copy-start(f32[768]{0:T(1024)S(1)} %get-tuple-element.272) | copy-start | bytes 9220
  105.1 7.4 %copy-start.81 = (f32[128]{0:T(128)}, f32[128]{0:T(128)S(1)}, u32[]{:S(2)}) copy-start(f32[128]{0:T(128)S(1)} %broadcast_divide_fusion.50) | copy-start | bytes 1540
  127.6 10.1 %collective-permute-start.1 = (bf16[128,768]{1,0:T(8,128)(2,1)S(1)}, bf16[128,768]{1,0:T(8,128)(2,1)S(1)}, u32[]{:S(2)}, u32[]{:S(2)}) collective-permute-start(bf16[128,768]{1,0:T(8,128)(2,1)S(1)} %fusion.91), channel_id=1, source_target_pairs={{0,8},{8,16},{16,24},{1,9},{9,17},{17,25},{2,10},{10,18},{18,26},{... | collective-permute-start | bytes 589832 | tf_op jit(solution)/shard_map/ppermute | solution.py:15
  132.9 8.8 %copy-start.33 = (f32[768]{0:T(1024)S(1)}, f32[768]{0:T(1024)}, u32[]{:S(2)}) copy-start(f32[768]{0:T(1024)} %fusion.717) | copy-start | bytes 9220
  134.1 8.1 %copy-start.67 = (f32[3072]{0:T(1024)S(1)}, f32[3072]{0:T(1024)}, u32[]{:S(2)}) copy-start(f32[3072]{0:T(1024)} %fusion.659) | copy-start | bytes 36868
  134.1 7.6 %collective-permute-start.2 = (bf16[128,768]{1,0:T(8,128)(2,1)S(1)}, bf16[128,768]{1,0:T(8,128)(2,1)S(1)}, u32[]{:S(2)}, u32[]{:S(2)}) collective-permute-start(bf16[128,768]{1,0:T(8,128)(2,1)S(1)} %fusion.92), channel_id=1, source_target_pairs={{0,8},{8,16},{16,24},{1,9},{9,17},{17,25},{2,10},{10,18},{18,26},{... | collective-permute-start | bytes 589832 | tf_op jit(solution)/shard_map/ppermute | solution.py:15
  145.3 11.8 %collective-permute-start.3 = (bf16[128,768]{1,0:T(8,128)(2,1)S(1)}, bf16[128,768]{1,0:T(8,128)(2,1)S(1)}, u32[]{:S(2)}, u32[]{:S(2)}) collective-permute-start(bf16[128,768]{1,0:T(8,128)(2,1)S(1)} %fusion.93), channel_id=1, source_target_pairs={{0,8},{8,16},{16,24},{1,9},{9,17},{17,25},{2,10},{10,18},{18,26},{... | collective-permute-start | bytes 589832 | tf_op jit(solution)/shard_map/ppermute | solution.py:15
  151.7 8.6 %copy-start.31 = (f32[768]{0:T(1024)S(1)}, f32[768]{0:T(1024)}, u32[]{:S(2)}) copy-start(f32[768]{0:T(1024)} %fusion.713) | copy-start | bytes 9220
  152.8 7.9 %copy-start.65 = (f32[3072]{0:T(1024)S(1)}, f32[3072]{0:T(1024)}, u32[]{:S(2)}) copy-start(f32[3072]{0:T(1024)} %fusion.661) | copy-start | bytes 36868
  152.8 7.4 %collective-permute-start.4 = (bf16[128,768]{1,0:T(8,128)(2,1)S(1)}, bf16[128,768]{1,0:T(8,128)(2,1)S(1)}, u32[]{:S(2)}, u32[]{:S(2)}) collective-permute-start(bf16[128,768]{1,0:T(8,128)(2,1)S(1)} %fusion.94), channel_id=1, source_target_pairs={{0,8},{8,16},{16,24},{1,9},{9,17},{17,25},{2,10},{10,18},{18,26},{... | collective-permute-start | bytes 589832 | tf_op jit(solution)/shard_map/ppermute | solution.py:15
  163.8 11.0 %collective-permute-start.5 = (bf16[128,768]{1,0:T(8,128)(2,1)S(1)}, bf16[128,768]{1,0:T(8,128)(2,1)S(1)}, u32[]{:S(2)}, u32[]{:S(2)}) collective-permute-start(bf16[128,768]{1,0:T(8,128)(2,1)S(1)} %fusion.95), channel_id=1, source_target_pairs={{0,8},{8,16},{16,24},{1,9},{9,17},{17,25},{2,10},{10,18},{18,26},{... | collective-permute-start | bytes 589832 | tf_op jit(solution)/shard_map/ppermute | solution.py:15
  170.6 7.3 %copy-start.29 = (f32[768]{0:T(1024)S(1)}, f32[768]{0:T(1024)}, u32[]{:S(2)}) copy-start(f32[768]{0:T(1024)} %fusion.709) | copy-start | bytes 9220
  171.7 6.6 %copy-start.63 = (f32[3072]{0:T(1024)S(1)}, f32[3072]{0:T(1024)}, u32[]{:S(2)}) copy-start(f32[3072]{0:T(1024)} %fusion.663) | copy-start | bytes 36868
  171.7 6.2 %collective-permute-start.6 = (bf16[128,768]{1,0:T(8,128)(2,1)S(1)}, bf16[128,768]{1,0:T(8,128)(2,1)S(1)}, u32[]{:S(2)}, u32[]{:S(2)}) collective-permute-start(bf16[128,768]{1,0:T(8,128)(2,1)S(1)} %fusion.96), channel_id=1, source_target_pairs={{0,8},{8,16},{16,24},{1,9},{9,17},{17,25},{2,10},{10,18},{18,26},{... | collective-permute-start | bytes 589832 | tf_op jit(solution)/shard_map/ppermute | solution.py:15
  181.5 10.5 %collective-permute-start.7 = (bf16[128,768]{1,0:T(8,128)(2,1)S(1)}, bf16[128,768]{1,0:T(8,128)(2,1)S(1)}, u32[]{:S(2)}, u32[]{:S(2)}) collective-permute-start(bf16[128,768]{1,0:T(8,128)(2,1)S(1)} %fusion.97), channel_id=1, source_target_pairs={{0,8},{8,16},{16,24},{1,9},{9,17},{17,25},{2,10},{10,18},{18,26},{... | collective-permute-start | bytes 589832 | tf_op jit(solution)/shard_map/ppermute | solution.py:15
  187.8 7.1 %copy-start.27 = (f32[768]{0:T(1024)S(1)}, f32[768]{0:T(1024)}, u32[]{:S(2)}) copy-start(f32[768]{0:T(1024)} %fusion.705) | copy-start | bytes 9220
  189.0 6.4 %copy-start.61 = (f32[3072]{0:T(1024)S(1)}, f32[3072]{0:T(1024)}, u32[]{:S(2)}) copy-start(f32[3072]{0:T(1024)} %fusion.665) | copy-start | bytes 36868
  189.0 6.0 %collective-permute-start.8 = (bf16[128,768]{1,0:T(8,128)(2,1)S(1)}, bf16[128,768]{1,0:T(8,128)(2,1)S(1)}, u32[]{:S(2)}, u32[]{:S(2)}) collective-permute-start(bf16[128,768]{1,0:T(8,128)(2,1)S(1)} %fusion.98), channel_id=1, source_target_pairs={{0,8},{8,16},{16,24},{1,9},{9,17},{17,25},{2,10},{10,18},{18,26},{... | collective-permute-start | bytes 589832 | tf_op jit(solution)/shard_map/ppermute | solution.py:15
  198.5 10.4 %collective-permute-start.9 = (bf16[128,768]{1,0:T(8,128)(2,1)S(1)}, bf16[128,768]{1,0:T(8,128)(2,1)S(1)}, u32[]{:S(2)}, u32[]{:S(2)}) collective-permute-start(bf16[128,768]{1,0:T(8,128)(2,1)S(1)} %fusion.99), channel_id=1, source_target_pairs={{0,8},{8,16},{16,24},{1,9},{9,17},{17,25},{2,10},{10,18},{18,26},{... | collective-permute-start | bytes 589832 | tf_op jit(solution)/shard_map/ppermute | solution.py:15
  204.9 7.1 %copy-start.25 = (f32[768]{0:T(1024)S(1)}, f32[768]{0:T(1024)}, u32[]{:S(2)}) copy-start(f32[768]{0:T(1024)} %fusion.701) | copy-start | bytes 9220
  206.0 6.4 %copy-start.59 = (f32[3072]{0:T(1024)S(1)}, f32[3072]{0:T(1024)}, u32[]{:S(2)}) copy-start(f32[3072]{0:T(1024)} %fusion.667) | copy-start | bytes 36868
  206.1 6.0 %collective-permute-start.10 = (bf16[128,768]{1,0:T(8,128)(2,1)S(1)}, bf16[128,768]{1,0:T(8,128)(2,1)S(1)}, u32[]{:S(2)}, u32[]{:S(2)}) collective-permute-start(bf16[128,768]{1,0:T(8,128)(2,1)S(1)} %fusion.100), channel_id=1, source_target_pairs={{0,8},{8,16},{16,24},{1,9},{9,17},{17,25},{2,10},{10,18},{18,26},{... | collective-permute-start | bytes 589832 | tf_op jit(solution)/shard_map/ppermute | solution.py:15
  215.5 10.6 %collective-permute-start.11 = (bf16[128,768]{1,0:T(8,128)(2,1)S(1)}, bf16[128,768]{1,0:T(8,128)(2,1)S(1)}, u32[]{:S(2)}, u32[]{:S(2)}) collective-permute-start(bf16[128,768]{1,0:T(8,128)(2,1)S(1)} %fusion.101), channel_id=1, source_target_pairs={{0,8},{8,16},{16,24},{1,9},{9,17},{17,25},{2,10},{10,18},{18,26},{... | collective-permute-start | bytes 589832 | tf_op jit(solution)/shard_map/ppermute | solution.py:15
  222.1 7.2 %copy-start.23 = (f32[768]{0:T(1024)S(1)}, f32[768]{0:T(1024)}, u32[]{:S(2)}) copy-start(f32[768]{0:T(1024)} %fusion.725) | copy-start | bytes 9220
  223.3 6.8 %copy-start.57 = (f32[3072]{0:T(1024)S(1)}, f32[3072]{0:T(1024)}, u32[]{:S(2)}) copy-start(f32[3072]{0:T(1024)} %fusion.669) | copy-start | bytes 36868
  223.3 6.0 %collective-permute-start.12 = (bf16[128,768]{1,0:T(8,128)(2,1)S(1)}, bf16[128,768]{1,0:T(8,128)(2,1)S(1)}, u32[]{:S(2)}, u32[]{:S(2)}) collective-permute-start(bf16[128,768]{1,0:T(8,128)(2,1)S(1)} %fusion.102), channel_id=1, source_target_pairs={{0,8},{8,16},{16,24},{1,9},{9,17},{17,25},{2,10},{10,18},{18,26},{... | collective-permute-start | bytes 589832 | tf_op jit(solution)/shard_map/ppermute | solution.py:15
  246.4 8.0 %collective-permute-start.15 = (bf16[128,768]{1,0:T(8,128)(2,1)S(1)}, bf16[128,768]{1,0:T(8,128)(2,1)S(1)}, u32[]{:S(2)}, u32[]{:S(2)}) collective-permute-start(bf16[128,768]{1,0:T(8,128)(2,1)S(1)} %get-tuple-element.107), channel_id=1, source_target_pairs={{8,0},{16,8},{24,16},{9,1},{17,9},{25,17},{10,2},{18,10},{26,18},{... | collective-permute-start | bytes 589832 | tf_op jit(solution)/shard_map/ppermute | solution.py:15
  258.2 9.1 %copy-start.54 = (f32[768]{0:T(1024)S(1)}, f32[768]{0:T(1024)}, u32[]{:S(2)}) copy-start(f32[768]{0:T(1024)} %fusion.688) | copy-start | bytes 9220
  258.8 8.5 %collective-permute-start.17 = (bf16[128,768]{1,0:T(8,128)(2,1)S(1)}, bf16[128,768]{1,0:T(8,128)(2,1)S(1)}, u32[]{:S(2)}, u32[]{:S(2)}) collective-permute-start(bf16[128,768]{1,0:T(8,128)(2,1)S(1)} %fusion.472), channel_id=1, source_target_pairs={{8,0},{16,8},{24,16},{9,1},{17,9},{25,17},{10,2},{18,10},{26,18},{... | collective-permute-start | bytes 589832 | tf_op jit(solution)/shard_map/ppermute | solution.py:15
  270.9 8.8 %copy-start.53 = (f32[768]{0:T(1024)S(1)}, f32[768]{0:T(1024)}, u32[]{:S(2)}) copy-start(f32[768]{0:T(1024)} %fusion.684) | copy-start | bytes 9220
  271.2 8.5 %collective-permute-start.19 = (bf16[128,768]{1,0:T(8,128)(2,1)S(1)}, bf16[128,768]{1,0:T(8,128)(2,1)S(1)}, u32[]{:S(2)}, u32[]{:S(2)}) collective-permute-start(bf16[128,768]{1,0:T(8,128)(2,1)S(1)} %fusion.476), channel_id=1, source_target_pairs={{8,0},{16,8},{24,16},{9,1},{17,9},{25,17},{10,2},{18,10},{26,18},{... | collective-permute-start | bytes 589832 | tf_op jit(solution)/shard_map/ppermute | solution.py:15
  283.3 8.8 %copy-start.52 = (f32[768]{0:T(1024)S(1)}, f32[768]{0:T(1024)}, u32[]{:S(2)}) copy-start(f32[768]{0:T(1024)} %fusion.680) | copy-start | bytes 9220
  283.6 8.5 %collective-permute-start.21 = (bf16[128,768]{1,0:T(8,128)(2,1)S(1)}, bf16[128,768]{1,0:T(8,128)(2,1)S(1)}, u32[]{:S(2)}, u32[]{:S(2)}) collective-permute-start(bf16[128,768]{1,0:T(8,128)(2,1)S(1)} %fusion.480), channel_id=1, source_target_pairs={{8,0},{16,8},{24,16},{9,1},{17,9},{25,17},{10,2},{18,10},{26,18},{... | collective-permute-start | bytes 589832 | tf_op jit(solution)/shard_map/ppermute | solution.py:15
  295.6 9.6 %copy-start.51 = (f32[768]{0:T(1024)S(1)}, f32[768]{0:T(1024)}, u32[]{:S(2)}) copy-start(f32[768]{0:T(1024)} %fusion.676) | copy-start | bytes 9220
  295.9 9.2 %collective-permute-start.23 = (bf16[128,768]{1,0:T(8,128)(2,1)S(1)}, bf16[128,768]{1,0:T(8,128)(2,1)S(1)}, u32[]{:S(2)}, u32[]{:S(2)}) collective-permute-start(bf16[128,768]{1,0:T(8,128)(2,1)S(1)} %fusion.484), channel_id=1, source_target_pairs={{8,0},{16,8},{24,16},{9,1},{17,9},{25,17},{10,2},{18,10},{26,18},{... | collective-permute-start | bytes 589832 | tf_op jit(solution)/shard_map/ppermute | solution.py:15
  305.2 13.9 %slice-start.2 = ((s8[7077888]{0:T(1024)(128)(4,1)}), s8[4194304]{0:T(1024)(128)(4,1)S(1)}, s32[]{:S(2)}) async-start(s8[7077888]{0:T(1024)(128)(4,1)} %bitcast.1036), calls=%async_computation.8 | async-start | bytes 8388608
  306.8 10.6 %copy-start.46 = (f32[768]{0:T(1024)S(1)}, f32[768]{0:T(1024)}, u32[]{:S(2)}) copy-start(f32[768]{0:T(1024)} %fusion.694) | copy-start | bytes 9220
  306.8 12.2 %slice-start.3 = ((s8[7077888]{0:T(1024)(128)(4,1)}), s8[2883584]{0:T(1024)(128)(4,1)S(1)}, s32[]{:S(2)}) async-start(s8[7077888]{0:T(1024)(128)(4,1)} %bitcast.1036), calls=%async_computation.9 | async-start | bytes 5767168
  309.0 8.4 %collective-permute-start.14 = (bf16[128,768]{1,0:T(8,128)(2,1)S(1)}, bf16[128,768]{1,0:T(8,128)(2,1)S(1)}, u32[]{:S(2)}, u32[]{:S(2)}) collective-permute-start(bf16[128,768]{1,0:T(8,128)(2,1)S(1)} %fusion.228), channel_id=1, source_target_pairs={{8,0},{16,8},{24,16},{9,1},{17,9},{25,17},{10,2},{18,10},{26,18},{... | collective-permute-start | bytes 589832 | tf_op jit(solution)/shard_map/ppermute | solution.py:15
  323.3 12.0 %copy-start.45 = (f32[768]{0:T(1024)S(1)}, f32[768]{0:T(1024)}, u32[]{:S(2)}) copy-start(f32[768]{0:T(1024)} %fusion.690) | copy-start | bytes 9220
  323.9 73.9 %collective-permute-start.25 = (bf16[128,768]{1,0:T(8,128)(2,1)S(1)}, bf16[128,768]{1,0:T(8,128)(2,1)S(1)}, u32[]{:S(2)}, u32[]{:S(2)}) collective-permute-start(bf16[128,768]{1,0:T(8,128)(2,1)S(1)} %get-tuple-element.104), channel_id=1, source_target_pairs={{8,0},{16,8},{24,16},{9,1},{17,9},{25,17},{10,2},{18,10},{26,18},{... | collective-permute-start | bytes 589832 | tf_op jit(solution)/shard_map/ppermute | solution.py:15
  325.2 10.1 %collective-permute-start.16 = (bf16[128,768]{1,0:T(8,128)(2,1)S(1)}, bf16[128,768]{1,0:T(8,128)(2,1)S(1)}, u32[]{:S(2)}, u32[]{:S(2)}) collective-permute-start(bf16[128,768]{1,0:T(8,128)(2,1)S(1)} %get-tuple-element.105), channel_id=1, source_target_pairs={{8,0},{16,8},{24,16},{9,1},{17,9},{25,17},{10,2},{18,10},{26,18},{... | collective-permute-start | bytes 589832 | tf_op jit(solution)/shard_map/ppermute | solution.py:15
  338.8 13.1 %copy-start.44 = (f32[768]{0:T(1024)S(1)}, f32[768]{0:T(1024)}, u32[]{:S(2)}) copy-start(f32[768]{0:T(1024)} %fusion.686) | copy-start | bytes 9220
  341.1 10.8 %collective-permute-start.18 = (bf16[128,768]{1,0:T(8,128)(2,1)S(1)}, bf16[128,768]{1,0:T(8,128)(2,1)S(1)}, u32[]{:S(2)}, u32[]{:S(2)}) collective-permute-start(bf16[128,768]{1,0:T(8,128)(2,1)S(1)} %fusion.474), channel_id=1, source_target_pairs={{8,0},{16,8},{24,16},{9,1},{17,9},{25,17},{10,2},{18,10},{26,18},{... | collective-permute-start | bytes 589832 | tf_op jit(solution)/shard_map/ppermute | solution.py:15
  355.3 11.4 %copy-start.43 = (f32[768]{0:T(1024)S(1)}, f32[768]{0:T(1024)}, u32[]{:S(2)}) copy-start(f32[768]{0:T(1024)} %fusion.682) | copy-start | bytes 9220
  357.5 9.3 %collective-permute-start.20 = (bf16[128,768]{1,0:T(8,128)(2,1)S(1)}, bf16[128,768]{1,0:T(8,128)(2,1)S(1)}, u32[]{:S(2)}, u32[]{:S(2)}) collective-permute-start(bf16[128,768]{1,0:T(8,128)(2,1)S(1)} %fusion.478), channel_id=1, source_target_pairs={{8,0},{16,8},{24,16},{9,1},{17,9},{25,17},{10,2},{18,10},{26,18},{... | collective-permute-start | bytes 589832 | tf_op jit(solution)/shard_map/ppermute | solution.py:15
  370.1 10.5 %copy-start.42 = (f32[768]{0:T(1024)S(1)}, f32[768]{0:T(1024)}, u32[]{:S(2)}) copy-start(f32[768]{0:T(1024)} %fusion.678) | copy-start | bytes 9220
  372.3 8.3 %collective-permute-start.22 = (bf16[128,768]{1,0:T(8,128)(2,1)S(1)}, bf16[128,768]{1,0:T(8,128)(2,1)S(1)}, u32[]{:S(2)}, u32[]{:S(2)}) collective-permute-start(bf16[128,768]{1,0:T(8,128)(2,1)S(1)} %fusion.482), channel_id=1, source_target_pairs={{8,0},{16,8},{24,16},{9,1},{17,9},{25,17},{10,2},{18,10},{26,18},{... | collective-permute-start | bytes 589832 | tf_op jit(solution)/shard_map/ppermute | solution.py:15
  384.0 10.4 %copy-start.41 = (f32[768]{0:T(1024)S(1)}, f32[768]{0:T(1024)}, u32[]{:S(2)}) copy-start(f32[768]{0:T(1024)} %fusion.674) | copy-start | bytes 9220
  386.1 8.3 %collective-permute-start.24 = (bf16[128,768]{1,0:T(8,128)(2,1)S(1)}, bf16[128,768]{1,0:T(8,128)(2,1)S(1)}, u32[]{:S(2)}, u32[]{:S(2)}) collective-permute-start(bf16[128,768]{1,0:T(8,128)(2,1)S(1)} %fusion.486), channel_id=1, source_target_pairs={{8,0},{16,8},{24,16},{9,1},{17,9},{25,17},{10,2},{18,10},{26,18},{... | collective-permute-start | bytes 589832 | tf_op jit(solution)/shard_map/ppermute | solution.py:15
  387.8 10.0 %copy-start.40 = (f32[768]{0:T(1024)S(1)}, f32[768]{0:T(1024)}, u32[]{:S(2)}) copy-start(f32[768]{0:T(1024)} %fusion.672) | copy-start | bytes 9220
  409.2 111.8 %reduce-scatter.5.cloned.1.call-start = ((), (), s32[]{:S(2)}) async-start(), calls=%async_computation.4 | async-start | bytes 5529600 | tf_op jit(solution)/shard_map/reduce_scatter | solution.py:184
  (57 other events, 184.6 us)
Sparse Core Ops, SparseCore 0:
  10.2 55.8 all-gather.3
  67.7 49.8 all-gather.5
  409.3 54.2 reduce-scatter.2
  465.7 55.1 reduce-scatter.4
where the time goes:
time: 542 us; the launch traced here: 531 us
  waiting for transfers between devices  189 us (35%)
  matrix products  116 us (21%)
  other arithmetic  75.4 us (14%)
  starting transfers between devices  69.7 us (13%)
  between operations  59.9 us (11%)
  local copies, waits for them, and re-layouts  21.9 us (4%)
    ppermute x26, waiting for transfers between devices, passed_along(): return lax.ppermute(block, axis, route)  97.3 us
    ppermute x26, starting transfers between devices, passed_along(): return lax.ppermute(block, axis, route)  69.5 us
    dot_general x28, matrix products, contract_last(): lax.dot_general(left, right, (((1,), (1,)), ((), ())), preferred_element_...  57.3 us
    reduce_scatter x1, waiting for transfers between devices, per_device(): own_down = lax.psum_scatter(packed, 'fsdp', scatter_dimension=0, tiled=True)  55.2 us
    reduce_scatter x1, waiting for transfers between devices, per_device(): own_up = lax.psum_scatter(part_up, 'fsdp', scatter_dimension=0, tiled=True)  33.2 us
    dot_general x14, matrix products, forward_tick(): hidden = jnp.dot(normed, weight_up, preferred_element_type=jnp.float32)  27.5 us
    dynamic_update_slice x36, other arithmetic, store_row(): return lax.dynamic_update_index_in_dim(stash, value, slot, 0)  18.5 us
    dot_general x2, matrix products, contract_rows(): lax.dot_general(left, right, (((0,), (0,)), ((), ())), preferred_element_...  17.2 us
  transfers between devices with their start and end apart: 30, of which 20 were waited for; matrix products, arithmetic and copies ran while one was open for 23% of the time, Pallas kernels for 0%

commit v1 on v0

v1 whole, which is shorter than its diff:
```python
import functools

import jax
import jax.numpy as jnp
from jax import lax
from jax.experimental import pallas as pl
from jax.experimental.pallas import tpu as pltpu
from jax.sharding import PartitionSpec as P

BLOCK = 128
EPSILON = 1e-05
SCALE = 0.7978845608028654
MESH = pl.DeviceIdType.MESH
VMEM_BYTES = 66 * 1024 * 1000
BF16 = jnp.bfloat16
F32 = jnp.float32


def gelu_and_slope(hidden):
    square = hidden * hidden
    tanh = jnp.tanh(hidden * (SCALE + (SCALE * 0.044715) * square))
    half = 0.5 + 0.5 * tanh
    rise = (hidden * (0.5 * SCALE + (0.5 * SCALE * 0.134145) * square)) * (1.0 - tanh * tanh)
    return (hidden * half, half + rise)


def contract_last(left, right):
    return lax.dot_general(left, right, (((1,), (1,)), ((), ())), preferred_element_type=F32)


def chunks(total, size):
    size = size if total % size == 0 else total
    return [(start, size) for start in range(0, total, size)]


def pipeline_kernel(
    section_count,
    patches,
    cotangent,
    embed,
    live,
    hidden_mask,
    width_inv,
    gain_ref,
    w_up,
    w_down,
    grad_up,
    grad_down,
    grad_gain,
    x_in,
    x_out,
    g_in,
    g_out,
    act,
    slope,
    normed_t,
    branch_t,
    fwd_send,
    fwd_recv,
    bwd_send,
    bwd_recv,
):
    me = lax.axis_index("section")
    is_first = me == 0
    is_last = me == section_count - 1
    micro_count, rows, features = patches.shape
    hidden_count = w_up.shape[1]

    barrier = pltpu.get_barrier_semaphore()

    @pl.when(jnp.logical_not(is_first))
    def _():
        pl.semaphore_signal(barrier, inc=1, device_id={"section": me - 1}, device_id_type=MESH)

    @pl.when(jnp.logical_not(is_last))
    def _():
        pl.semaphore_signal(barrier, inc=1, device_id={"section": me + 1}, device_id_type=MESH)

    ends = is_first.astype(jnp.int32) + is_last.astype(jnp.int32)
    pl.semaphore_wait(barrier, 2 - ends)

    def forward_copy(m):
        return pltpu.make_async_remote_copy(
            src_ref=x_out.at[m],
            dst_ref=x_in.at[m],
            send_sem=fwd_send.at[m],
            recv_sem=fwd_recv.at[m],
            device_id={"section": jnp.minimum(me + 1, section_count - 1)},
            device_id_type=MESH,
        )

    def backward_copy(m):
        return pltpu.make_async_remote_copy(
            src_ref=g_out.at[m],
            dst_ref=g_in.at[m],
            send_sem=bwd_send.at[m],
            recv_sem=bwd_recv.at[m],
            device_id={"section": jnp.maximum(me - 1, 0)},
            device_id_type=MESH,
        )

    def layer_norm(m):
        mask = embed[m]
        scale = width_inv[m][:, :1]
        values = x_in[m].astype(F32) * mask
        center = jnp.sum(values, axis=-1, keepdims=True) * scale
        centered = (values - center) * mask
        variance = jnp.sum(centered * centered, axis=-1, keepdims=True) * scale
        inv_std = lax.rsqrt(variance + EPSILON)
        return centered * inv_std, inv_std

    gain = gain_ref[...]

    def forward(m, carry):
        at = pl.ds(pl.multiple_of(m * rows, rows), rows)

        @pl.when(is_first)
        def _():
            x_in[m] = (patches[m].astype(F32) * embed[m]).astype(BF16)

        @pl.when(jnp.logical_not(is_first))
        def _():
            forward_copy(m).wait_recv()

        standard, _ = layer_norm(m)
        scaled = standard * gain
        normed = scaled.astype(BF16)
        normed_t[:, at] = jnp.transpose(scaled).astype(BF16)
        for start, size in chunks(hidden_count, 512):
            part = pl.ds(start, size)
            hidden = jnp.dot(normed, w_up[:, part], preferred_element_type=F32)
            value, rise = gelu_and_slope(hidden)
            mask = hidden_mask[m, :, part]
            act[at, part] = (value * mask).astype(BF16)
            slope[at, part] = (rise * mask).astype(BF16)

        @pl.when(jnp.logical_not(is_last))
        def _():
            for start, size in chunks(features, 256):
                part = pl.ds(start, size)
                branch = jnp.dot(act[at, :], w_down[:, part], preferred_element_type=F32)
                out = x_in[m, :, part].astype(F32) + live[m, :, part] * branch
                x_out[m, :, part] = out.astype(BF16)
            forward_copy(m).start()

        return carry

    lax.fori_loop(0, micro_count, forward, 0)
    grad_gain[...] = jnp.zeros_like(grad_gain)

    def backward(m, carry):
        at = pl.ds(pl.multiple_of(m * rows, rows), rows)

        @pl.when(is_last)
        def _():
            g_in[m] = (cotangent[m].astype(F32) * embed[m]).astype(BF16)

        @pl.when(jnp.logical_not(is_last))
        def _():
            backward_copy(m).wait_recv()

        grad_float = g_in[m].astype(F32)
        branch_float = grad_float * live[m]
        branch = branch_float.astype(BF16)
        branch_t[:, at] = jnp.transpose(branch_float).astype(BF16)
        for start, size in chunks(hidden_count, 512):
            part = pl.ds(start, size)
            grad_act = contract_last(branch, w_down[part, :])
            slope[at, part] = (grad_act * slope[at, part].astype(F32)).astype(BF16)
        grad_hidden = slope[at, :]
        grad_normed = jnp.concatenate(
            [
                contract_last(grad_hidden, w_up[pl.ds(start, size), :])
                for start, size in chunks(features, 256)
            ],
            axis=1,
        )
        standard, inv_std = layer_norm(m)
        mask = embed[m]
        scale = width_inv[m][:, :1]
        grad_gain[...] += jnp.sum(grad_normed * standard, axis=0, keepdims=True)

        @pl.when(jnp.logical_not(is_first))
        def _():
            grad_standard = grad_normed * gain * mask
            first = jnp.sum(grad_standard, axis=-1, keepdims=True) * scale
            second = jnp.sum(grad_standard * standard, axis=-1, keepdims=True) * scale
            grad_x = inv_std * (grad_standard - first * mask - standard * second)
            g_out[m] = (grad_float + grad_x).astype(BF16)
            backward_copy(m).start()

        return carry

    lax.fori_loop(0, micro_count, backward, 0)

    width = 256 if hidden_count % 256 == 0 else hidden_count

    def weight_grads(step, carry):
        part = pl.ds(pl.multiple_of(step * width, width), width)
        up = jnp.dot(normed_t[...], slope[:, part], preferred_element_type=F32)
        grad_up[:, part] = up.astype(BF16)
        down = jnp.dot(branch_t[...], act[:, part], preferred_element_type=F32)
        grad_down[part, :] = jnp.transpose(down).astype(BF16)
        return carry

    lax.fori_loop(0, hidden_count // width, weight_grads, 0)

    def drain(m, carry):
        @pl.when(jnp.logical_not(is_last))
        def _():
            forward_copy(m).wait_send()

        @pl.when(jnp.logical_not(is_first))
        def _():
            backward_copy(m).wait_send()

        return carry

    lax.fori_loop(0, micro_count, drain, 0)


def run_pipeline(patches, cotangent, embed, live, hidden_mask, width_inv, gain, w_up, w_down):
    section_count = lax.axis_size("section")
    micro_count, rows, features = patches.shape
    hidden_count = w_up.shape[1]
    vmem = pl.BlockSpec(memory_space=pltpu.VMEM)
    token = (micro_count, rows, features)
    tokens = micro_count * rows
    return pl.pallas_call(
        functools.partial(pipeline_kernel, section_count),
        out_shape=(
            jax.ShapeDtypeStruct((features, hidden_count), BF16),
            jax.ShapeDtypeStruct((hidden_count, features), BF16),
            jax.ShapeDtypeStruct((1, features), F32),
        ),
        in_specs=[vmem] * 9,
        out_specs=(vmem, vmem, vmem),
        scratch_shapes=[
            pltpu.VMEM(token, BF16),
            pltpu.VMEM(token, BF16),
            pltpu.VMEM(token, BF16),
            pltpu.VMEM(token, BF16),
            pltpu.VMEM((tokens, hidden_count), BF16),
            pltpu.VMEM((tokens, hidden_count), BF16),
            pltpu.VMEM((features, tokens), BF16),
            pltpu.VMEM((features, tokens), BF16),
            pltpu.SemaphoreType.DMA((micro_count,)),
            pltpu.SemaphoreType.DMA((micro_count,)),
            pltpu.SemaphoreType.DMA((micro_count,)),
            pltpu.SemaphoreType.DMA((micro_count,)),
        ],
        compiler_params=pltpu.CompilerParams(
            collective_id=0, has_side_effects=True, vmem_limit_bytes=VMEM_BYTES
        ),
    )(patches, cotangent, embed, live, hidden_mask, width_inv, gain, w_up, w_down)


def per_device(patches, cotangent, embed_blocks, ratio_index, depth, w_up, w_down, ln_gain):
    section_index = lax.axis_index("section")
    micro_count, rows, features = patches.shape
    hidden_count = w_up.shape[2]

    width = embed_blocks * BLOCK
    hidden_width = width * (6 + ratio_index) // 2
    embed = (lax.iota(jnp.int32, features)[None, :] < width[:, None]).astype(F32)
    hidden_mask = (lax.iota(jnp.int32, hidden_count)[None, :] < hidden_width[:, None]).astype(F32)
    active = (section_index < depth).astype(F32)
    live = embed * active[:, None]
    width_inv = jnp.broadcast_to((1.0 / width.astype(F32))[:, None, None], (micro_count, 1, BLOCK))

    full_up = lax.all_gather(w_up[0], "fsdp", axis=0, tiled=True)
    full_down = lax.all_gather(w_down[0], "fsdp", axis=0, tiled=True)
    gain = lax.all_gather(ln_gain[0], "fsdp", axis=0, tiled=True).astype(F32)

    part_up, part_down, part_gain = run_pipeline(
        patches,
        cotangent,
        embed[:, None, :],
        live[:, None, :],
        hidden_mask[:, None, :],
        width_inv,
        gain[None],
        full_up,
        full_down,
    )
    own_down = lax.psum_scatter(part_down, "fsdp", scatter_dimension=0, tiled=True)
    own_up = lax.psum_scatter(part_up, "fsdp", scatter_dimension=0, tiled=True)
    own_gain = lax.psum_scatter(part_gain[0], "fsdp", scatter_dimension=0, tiled=True)
    return (own_up.astype(F32)[None], own_down.astype(F32)[None], own_gain[None])


def solution(mesh):
    return jax.shard_map(
        per_device,
        mesh=mesh,
        in_specs=(
            P(None, "fsdp", None),
            P(None, "fsdp", None),
            P(),
            P(),
            P(),
            P("section", "fsdp", None),
            P("section", "fsdp", None),
            P("section", "fsdp"),
        ),
        out_specs=(P("section", "fsdp", None), P("section", "fsdp", None), P("section", "fsdp")),
        check_vma=False,
    )
```

time: 542 us -> 372 us (0.69); the launches traced: 531 us -> 371 us
  Pallas kernels: 0 us -> 139 us
  matrix products: 116 us -> 0 us
  starting transfers between devices: 69.7 us -> 0.16 us
  other arithmetic: 75.4 us -> 8.5 us
  between operations: 59.9 us -> 15.1 us
  blocking collectives: 0 us -> 33.1 us
  local copies, waits for them, and re-layouts: 21.9 us -> 4.03 us
  waiting for transfers between devices: 189 us -> 172 us
    pallas_call x0 -> x1, Pallas kernels: none -> 139 us  [run_pipeline(): pl.pallas_call(functools.partial(pipeline_kernel, section_count), out_sha...]
    dot_general x56 -> x0, matrix products: 116 us -> none  [the longest x28 57.3 us: contract_last(): lax.dot_general(left, right, (((1,), (1,)), ((), ())), preferred_element_...]
    ppermute x26 -> x0, waiting for transfers between devices: 97.3 us -> none  [passed_along(): return lax.ppermute(block, axis, route)]
    all_gather x2, waiting for transfers between devices: 3.03 us -> 80.5 us  [the longest x1 51.6 us: per_device(): full_down = lax.all_gather(w_down[0], 'fsdp', axis=0, tiled=True)]
    ppermute x26 -> x0, starting transfers between devices: 69.5 us -> none  [passed_along(): return lax.ppermute(block, axis, route)]
    unnamed x0 -> x2, blocking collectives: none -> 33.1 us
    convert_element_type x51 -> x3, other arithmetic: 24.8 us -> 2.11 us  [the longest x1 0.76 us: per_device(): (lax.iota(jnp.int32, hidden_count)[None, :] < hidden_width[:, None]).asty...]
    reduce_scatter x1, waiting for transfers between devices: 33.2 us -> 53.1 us  [per_device(): own_up = lax.psum_scatter(part_up, 'fsdp', scatter_dimension=0, tiled=True)]
  transfers between devices with their start and end apart: 30 -> 4, of which waited for: 20 -> 4; matrix products, arithmetic and copies ran while one was open for 23% -> 3% of each run, Pallas kernels for 0% -> 0%
where the time goes in v1:
time: 372 us; the launch traced here: 371 us
  waiting for transfers between devices  172 us (46%)
  Pallas kernels  139 us (37%)
  blocking collectives  33.1 us (9%)
  between operations  15.1 us (4%)
  other arithmetic  8.5 us (2%)
  local copies, waits for them, and re-layouts  4.03 us (1%)
    pallas_call x1, Pallas kernels, run_pipeline(): pl.pallas_call(functools.partial(pipeline_kernel, section_count), out_sha...  139 us
    reduce_scatter x1, waiting for transfers between devices, per_device(): own_up = lax.psum_scatter(part_up, 'fsdp', scatter_dimension=0, tiled=True)  53.1 us
    all_gather x1, waiting for transfers between devices, per_device(): full_down = lax.all_gather(w_down[0], 'fsdp', axis=0, tiled=True)  51.6 us
    reduce_scatter x1, waiting for transfers between devices, per_device(): lax.psum_scatter(part_down, 'fsdp', scatter_dimension=0, tiled=True)  36.2 us
    unnamed x2, blocking collectives  33.1 us
    all_gather x1, waiting for transfers between devices, per_device(): full_up = lax.all_gather(w_up[0], 'fsdp', axis=0, tiled=True)  28.9 us
  transfers between devices with their start and end apart: 4, of which 4 were waited for; matrix products, arithmetic and copies ran while one was open for 3% of the time, Pallas kernels for 0%

profile of v1, /device:TPU:0, one launch (start us, length us, event | category | flops | bytes accessed | tf_op | source)
XLA Modules:
  0.0 371.4 jit_solution(8193657194180261770)
XLA Ops:
  7.2 0.0 all-gather.6.cloned.1.call-start
  7.2 0.7 all-gather.6.cloned.1.call-update
  7.9 0.0 all-gather.8.cloned.1.call-start
  7.9 0.7 all-gather.8.cloned.1.call-update
  8.6 0.0 reduce-scatter.5.cloned.1.call-start
  8.7 1.3 fusion
  10.7 0.8 dynamic-update-slice
  11.5 18.8 %all-reduce = bf16[768]{0:T(1024)(128)(2,1)S(1)} all-reduce(bf16[768]{0:T(1024)(128)(2,1)S(1)} %dynamic-update-slice), channel_id=2, replica_groups=mesh['section'=4,'fsdp'=8] {'fsdp'}, use_global_device_ids=true, to_apply=%add | all-reduce | flops 768 | bytes 3072
  30.4 0.6 reshape.120.gain_ref
  31.0 0.7 convert_divide_fusion
  31.6 0.7 compare_convert_fusion.2
  32.3 0.7 and_select_fusion
  33.0 0.7 compare_convert_fusion.1.embed
  33.7 0.7 compare_select_fusion.live
  34.4 0.8 compare_convert_fusion.hidden_mask
  35.1 28.9 %all-gather.6.cloned.1.call-done = bf16[1,768,3072]{2,1,0:T(8,128)(2,1)} async-done(((bf16[1,96,3072]{2,1,0:T(8,128)(2,1)}), bf16[1,768,3072]{2,1,0:T(8,128)(2,1)}) %all-gather.6.cloned.1.call-update) | async-done | bytes 4718608 | tf_op jit(solution)/shard_map/all_gather | solution.py:271
  64.1 51.6 %all-gather.8.cloned.1.call-done = bf16[1,3072,768]{2,1,0:T(8,128)(2,1)} async-done(((bf16[1,384,768]{2,1,0:T(8,128)(2,1)}), bf16[1,3072,768]{2,1,0:T(8,128)(2,1)}) %all-gather.8.cloned.1.call-update) | async-done | bytes 4718608 | tf_op jit(solution)/shard_map/all_gather | solution.py:272
  115.7 0.7 broadcast_in_dim.34.width_inv
  116.3 138.8 %shard_map.103 = (bf16[768,3072]{1,0:T(8,128)(2,1)}, bf16[3072,768]{1,0:T(8,128)(2,1)}, f32[1,768]{1,0:T(1,128)}) custom-call(bf16[8,128,768]{2,1,0:T(8,128)(2,1)} %patches.1, bf16[8,128,768]{2,1,0:T(8,128)(2,1)} %cotangent.1, f32[8,1,768]{2,1,0:T(1,128)} %compare_convert_fusion.1.embed, f32[8,1,768]{2,1,0:T(1,128)} %compare_select_fusion.live, ...), custom_call_target="tpu_custom_call" | custom-call | tf_op jit(solution)/shard_map/pallas_call | solution.py:229
  255.2 0.0 reduce-scatter.5.cloned.1.call-update
  255.2 0.0 reduce-scatter.3.cloned.1.call-start
  255.2 0.0 copy-start
  255.2 0.5 reduce-scatter.3.cloned.1.call-update
  256.4 0.0 copy-done
  256.4 14.2 %all-reduce.1 = f32[768]{0:T(1024)S(1)} all-reduce(f32[768]{0:T(1024)S(1)} %reduce), channel_id=7, replica_groups=mesh['section'=4,'fsdp'=8] {'fsdp'}, use_global_device_ids=true, to_apply=%region_2.3.clone | all-reduce | flops 768 | bytes 6144
  270.7 0.6 dynamic-slice_bitcast_fusion
  271.3 36.2 %reduce-scatter.5.cloned.1.call-done = bf16[384,768]{1,0:T(8,128)(2,1)} async-done(((bf16[3072,768]{1,0:T(8,128)(2,1)}), bf16[384,768]{1,0:T(8,128)(2,1)}) %reduce-scatter.5.cloned.1.call-update) | async-done | bytes 589840 | tf_op jit(solution)/shard_map/reduce_scatter | solution.py:286
  307.4 2.2 bitcast_convert_fusion
  309.6 53.1 %reduce-scatter.3.cloned.1.call-done = bf16[96,3072]{1,0:T(8,128)(2,1)} async-done(((bf16[768,3072]{1,0:T(8,128)(2,1)}), bf16[96,3072]{1,0:T(8,128)(2,1)}) %reduce-scatter.3.cloned.1.call-update) | async-done | bytes 589840 | tf_op jit(solution)/shard_map/reduce_scatter | solution.py:287
  362.7 2.2 bitcast_convert_fusion.1
  (2 shorter events, 0.0 us)
Async XLA Ops:
  7.2 56.9 %all-gather.6.cloned.1.call-start = ((), (), s32[]{:S(2)}) async-start(), calls=%async_computation.4 | async-start | bytes 5308416 | tf_op jit(solution)/shard_map/all_gather | solution.py:271
  7.9 107.8 %all-gather.8.cloned.1.call-start = ((), (), s32[]{:S(2)}) async-start(), calls=%async_computation.5 | async-start | bytes 5308416 | tf_op jit(solution)/shard_map/all_gather | solution.py:272
  8.6 298.8 %reduce-scatter.5.cloned.1.call-start = ((), (), s32[]{:S(2)}) async-start(), calls=%async_computation.3 | async-start | bytes 5308416 | tf_op jit(solution)/shard_map/reduce_scatter | solution.py:286
  255.2 107.5 %reduce-scatter.3.cloned.1.call-start = ((), (), s32[]{:S(2)}) async-start(), calls=%async_computation.2 | async-start | bytes 5308416 | tf_op jit(solution)/shard_map/reduce_scatter | solution.py:287
  255.2 1.2 copy-start
Sparse Core Ops, SparseCore 0:
  9.6 54.3 all-gather.5
  65.7 49.9 all-gather.7
  255.3 52.0 reduce-scatter.4
  309.6 53.0 reduce-scatter.2

commit v2 on v1

--- a/solution.py
+++ b/solution.py
@@ -1,4 +1,5 @@
 import functools
+import math
 
 import jax
 import jax.numpy as jnp
@@ -33,17 +34,22 @@
     return [(start, size) for start in range(0, total, size)]
 
 
+def signal(semaphore, device):
+    pl.semaphore_signal(semaphore, inc=1, device_id=device, device_id_type=MESH)
+
+
 def pipeline_kernel(
     section_count,
+    shard_count,
     patches,
     cotangent,
     embed,
     live,
     hidden_mask,
     width_inv,
-    gain_ref,
-    w_up,
-    w_down,
+    own_gain,
+    own_up,
+    own_down,
     grad_up,
     grad_down,
     grad_gain,
@@ -59,25 +65,159 @@
     fwd_recv,
     bwd_send,
     bwd_recv,
+    w_up=None,
+    w_down=None,
+    all_gain=None,
+    all_rise=None,
+    acc_gain=None,
+    pair_up=None,
+    pair_down=None,
+    line_up=None,
+    line_down=None,
+    spread_line_send=None,
+    spread_line_recv=None,
+    spread_pair_send=None,
+    spread_pair_recv=None,
+    sum_line_send=None,
+    sum_line_recv=None,
+    sum_pair_send=None,
+    sum_pair_recv=None,
 ):
+    inside = w_up is not None
     me = lax.axis_index("section")
     is_first = me == 0
     is_last = me == section_count - 1
     micro_count, rows, features = patches.shape
-    hidden_count = w_up.shape[1]
+    shard = lax.axis_index("fsdp")
+    chip = shard // 2
+    core = shard % 2
+    chips = shard_count // 2
+    has_below = chip > 0
+    has_above = chip < chips - 1
+    other = shard + 1 - 2 * core
 
     barrier = pltpu.get_barrier_semaphore()
 
     @pl.when(jnp.logical_not(is_first))
     def _():
-        pl.semaphore_signal(barrier, inc=1, device_id={"section": me - 1}, device_id_type=MESH)
+        signal(barrier, {"section": me - 1})
 
     @pl.when(jnp.logical_not(is_last))
     def _():
-        pl.semaphore_signal(barrier, inc=1, device_id={"section": me + 1}, device_id_type=MESH)
-
-    ends = is_first.astype(jnp.int32) + is_last.astype(jnp.int32)
-    pl.semaphore_wait(barrier, 2 - ends)
+        signal(barrier, {"section": me + 1})
+
+    peers = 2 - is_first.astype(jnp.int32) - is_last.astype(jnp.int32)
+    if inside:
+        signal(barrier, {"fsdp": other})
+
+        @pl.when(has_below)
+        def _():
+            signal(barrier, {"fsdp": shard - 2})
+
+        @pl.when(has_above)
+        def _():
+            signal(barrier, {"fsdp": shard + 2})
+
+        peers = peers + 1 + has_below.astype(jnp.int32) + has_above.astype(jnp.int32)
+    pl.semaphore_wait(barrier, peers)
+
+    def slot(full, index):
+        if full.ndim == 3:
+            return full.at[index]
+        size = full.shape[0] // shard_count
+        return full.at[pl.ds(pl.multiple_of(index * size, size), size)]
+
+    def line_copy(full, number, source, place, step):
+        return pltpu.make_async_remote_copy(
+            src_ref=source,
+            dst_ref=slot(full, 2 * place + core),
+            send_sem=spread_line_send.at[number, (step + 1) // 2, place],
+            recv_sem=spread_line_recv.at[number, place],
+            device_id={"fsdp": jnp.clip(shard + 2 * step, 0, shard_count - 1)},
+            device_id_type=MESH,
+        )
+
+    def pair_copy(full, number, source, place):
+        return pltpu.make_async_remote_copy(
+            src_ref=source,
+            dst_ref=slot(full, 2 * place + core),
+            send_sem=spread_pair_send.at[number, place],
+            recv_sem=spread_pair_recv.at[number, place],
+            device_id={"fsdp": other},
+            device_id_type=MESH,
+        )
+
+    def spread_open(full, number, own):
+        @pl.when(has_above)
+        def _():
+            line_copy(full, number, own, chip, 1).start()
+
+        @pl.when(has_below)
+        def _():
+            line_copy(full, number, own, chip, -1).start()
+
+        pair_copy(full, number, own, chip).start()
+        mine = slot(full, shard)
+        mine[...] = own[...]
+
+    def spread_step(full, number, distance):
+        below = jnp.maximum(chip - distance, 0)
+        above = jnp.minimum(chip + distance, chips - 1)
+
+        @pl.when(chip >= distance)
+        def _():
+            source = slot(full, 2 * below + core)
+            line_copy(full, number, source, below, 1).wait_recv()
+
+            @pl.when(has_above)
+            def _():
+                line_copy(full, number, source, below, 1).start()
+
+            pair_copy(full, number, source, below).start()
+
+        @pl.when(chip + distance < chips)
+        def _():
+            source = slot(full, 2 * above + core)
+            line_copy(full, number, source, above, -1).wait_recv()
+
+            @pl.when(has_below)
+            def _():
+                line_copy(full, number, source, above, -1).start()
+
+            pair_copy(full, number, source, above).start()
+
+    def spread_close(full, number):
+        for place in range(chips):
+            source = slot(full, 2 * place + core)
+            pair_copy(full, number, source, place).wait_recv()
+
+    def spread_sent(full, number):
+        for place in range(chips):
+            source = slot(full, 2 * place + core)
+            pair_copy(full, number, source, place).wait_send()
+
+            @pl.when(jnp.logical_and(place <= chip, has_above))
+            def _():
+                line_copy(full, number, source, place, 1).wait_send()
+
+            @pl.when(jnp.logical_and(place >= chip, has_below))
+            def _():
+                line_copy(full, number, source, place, -1).wait_send()
+
+    if inside:
+        loads = ((w_up, 0, own_up), (w_down, 1, own_down), (all_gain, 2, own_gain))
+        for full, number, own in loads:
+            spread_open(full, number, own)
+        for distance in range(1, chips):
+            for full, number, own in loads:
+                spread_step(full, number, distance)
+        for full, number, own in loads:
+            spread_close(full, number)
+        gain = jnp.sum(all_gain[...], axis=0)[:1]
+    else:
+        w_up, w_down, acc_gain = own_up, own_down, grad_gain
+        gain = own_gain[:1]
+    hidden_count = w_up.shape[1]
 
     def forward_copy(m):
         return pltpu.make_async_remote_copy(
@@ -108,8 +248,6 @@
         variance = jnp.sum(centered * centered, axis=-1, keepdims=True) * scale
         inv_std = lax.rsqrt(variance + EPSILON)
         return centered * inv_std, inv_std
-
-    gain = gain_ref[...]
 
     def forward(m, carry):
         at = pl.ds(pl.multiple_of(m * rows, rows), rows)
@@ -146,7 +284,7 @@
         return carry
 
     lax.fori_loop(0, micro_count, forward, 0)
-    grad_gain[...] = jnp.zeros_like(grad_gain)
+    acc_gain[...] = jnp.zeros_like(acc_gain)
 
     def backward(m, carry):
         at = pl.ds(pl.multiple_of(m * rows, rows), rows)
@@ -178,7 +316,7 @@
         standard, inv_std = layer_norm(m)
         mask = embed[m]
         scale = width_inv[m][:, :1]
-        grad_gain[...] += jnp.sum(grad_normed * standard, axis=0, keepdims=True)
+        acc_gain[...] += jnp.sum((grad_normed * standard).reshape(-1, 8, features), axis=0)
 
         @pl.when(jnp.logical_not(is_first))
         def _():
@@ -195,15 +333,138 @@
 
     width = 256 if hidden_count % 256 == 0 else hidden_count
 
+    def up_grads(first, size, step):
+        part = pl.ds(pl.multiple_of(step * width, width), width)
+        these = pl.ds(first, size)
+        return these, part, jnp.dot(normed_t[these, :], slope[:, part], preferred_element_type=F32)
+
+    def down_grads(part):
+        down = jnp.dot(branch_t[...], act[:, part], preferred_element_type=F32)
+        return jnp.transpose(down).astype(BF16)
+
     def weight_grads(step, carry):
-        part = pl.ds(pl.multiple_of(step * width, width), width)
-        up = jnp.dot(normed_t[...], slope[:, part], preferred_element_type=F32)
-        grad_up[:, part] = up.astype(BF16)
-        down = jnp.dot(branch_t[...], act[:, part], preferred_element_type=F32)
-        grad_down[part, :] = jnp.transpose(down).astype(BF16)
+        these, part, up = up_grads(0, features, step)
+        grad_up[these, part] = up.astype(BF16)
+        grad_down[part, :] = down_grads(part)
         return carry
 
-    lax.fori_loop(0, hidden_count // width, weight_grads, 0)
+    def sum_pair(full, pair, number, place):
+        return pltpu.make_async_remote_copy(
+            src_ref=slot(full, 2 * place + 1 - core),
+            dst_ref=pair.at[place],
+            send_sem=sum_pair_send.at[number, place],
+            recv_sem=sum_pair_recv.at[number, place],
+            device_id={"fsdp": other},
+            device_id_type=MESH,
+        )
+
+    def sum_line(full, line, number, place, target, to):
+        return pltpu.make_async_remote_copy(
+            src_ref=slot(full, 2 * place + core),
+            dst_ref=line.at[target],
+            send_sem=sum_line_send.at[number, place],
+            recv_sem=sum_line_recv.at[number, target],
+            device_id={"fsdp": to},
+            device_id_type=MESH,
+        )
+
+    def reduce_step(index, carry):
+        distance = chips - 1 - index // 2
+        way = 1 - 2 * (index % 2)
+        place = chip + way * distance
+
+        for hops in range(1, chips):
+
+            @pl.when(index == 2 * hops)
+            def _():
+                spread_step(all_rise, 3, hops)
+
+        @pl.when(jnp.logical_and(place >= 0, place < chips))
+        def _():
+            up_size = 2 * features // shard_count
+            first_row = pl.multiple_of(place * up_size, up_size)
+
+            def up_part(step, carry):
+                these, part, up = up_grads(first_row, up_size, step)
+                w_up[these, part] = up.astype(BF16)
+                return carry
+
+            lax.fori_loop(0, hidden_count // width, up_part, 0)
+            sum_pair(w_up, pair_up, 0, place).start()
+            down_size = 2 * hidden_count // shard_count
+
+            def down_part(step, carry):
+                piece = math.gcd(down_size, width)
+                part = pl.ds(pl.multiple_of(place * down_size + step * piece, piece), piece)
+                w_down[part, :] = down_grads(part)
+                return carry
+
+            lax.fori_loop(0, down_size // math.gcd(down_size, width), down_part, 0)
+            sum_pair(w_down, pair_down, 1, place).start()
+
+            is_own = distance == 0
+            from_below = jnp.logical_and(place >= chip, has_below)
+            from_above = jnp.logical_and(place <= chip, has_above)
+            high_slot = jnp.where(is_own, chips, place)
+            to = jnp.clip(shard + 2 * way, 0, shard_count - 1)
+            target = jnp.where(place == chip - 1, chips, place)
+            sets = ((w_up, pair_up, line_up, 0, grad_up), (w_down, pair_down, line_down, 1, grad_down))
+            for full, pair, line, number, out in sets:
+                mine = slot(full, 2 * place + core)
+                sum_pair(full, pair, number, place).wait_recv()
+
+                @pl.when(from_below)
+                def _():
+                    sum_line(full, line, number, place, place, to).wait_recv()
+
+                @pl.when(from_above)
+                def _():
+                    sum_line(full, line, number, place, high_slot, to).wait_recv()
+
+                @pl.when(jnp.logical_not(is_own))
+                def _():
+                    @pl.when(jnp.logical_or(from_below, from_above))
+                    def _():
+                        total = mine[...].astype(F32) + pair[place].astype(F32)
+                        mine[...] = (total + line[place].astype(F32)).astype(BF16)
+
+                    @pl.when(jnp.logical_not(jnp.logical_or(from_below, from_above)))
+                    def _():
+                        mine[...] = (mine[...].astype(F32) + pair[place].astype(F32)).astype(BF16)
+
+                    sum_line(full, line, number, place, target, to).start()
+
+                @pl.when(is_own)
+                def _():
+                    out[...] = mine[...].astype(F32) + pair[place].astype(F32)
+
+                    @pl.when(from_below)
+                    def _():
+                        out[...] += line[place].astype(F32)
+
+                    @pl.when(from_above)
+                    def _():
+                        out[...] += line[chips].astype(F32)
+
+        return carry
+
+    if inside:
+        spread_open(all_rise, 3, acc_gain)
+        for full, number, own in loads:
+            spread_sent(full, number)
+        lax.fori_loop(0, 2 * chips - 1, reduce_step, 0)
+        spread_close(all_rise, 3)
+        spread_sent(all_rise, 3)
+        grad_gain[...] = jnp.sum(all_rise[...], axis=0)
+        for place in range(chips):
+            for full, pair, line, number in ((w_up, pair_up, line_up, 0), (w_down, pair_down, line_down, 1)):
+                sum_pair(full, pair, number, place).wait_send()
+
+                @pl.when(chip != place)
+                def _():
+                    sum_line(full, line, number, place, place, other).wait_send()
+    else:
+        lax.fori_loop(0, hidden_count // width, weight_grads, 0)
 
     def drain(m, carry):
         @pl.when(jnp.logical_not(is_last))
@@ -219,36 +480,66 @@
     lax.fori_loop(0, micro_count, drain, 0)
 
 
-def run_pipeline(patches, cotangent, embed, live, hidden_mask, width_inv, gain, w_up, w_down):
+def run_pipeline(inside, patches, cotangent, embed, live, hidden_mask, width_inv, gain, w_up, w_down):
     section_count = lax.axis_size("section")
+    shard_count = lax.axis_size("fsdp")
     micro_count, rows, features = patches.shape
     hidden_count = w_up.shape[1]
     vmem = pl.BlockSpec(memory_space=pltpu.VMEM)
     token = (micro_count, rows, features)
     tokens = micro_count * rows
-    return pl.pallas_call(
-        functools.partial(pipeline_kernel, section_count),
-        out_shape=(
+    chips = shard_count // 2
+    dma = pltpu.SemaphoreType.DMA
+    scratch = [
+        pltpu.VMEM(token, BF16),
+        pltpu.VMEM(token, BF16),
+        pltpu.VMEM(token, BF16),
+        pltpu.VMEM(token, BF16),
+        pltpu.VMEM((tokens, hidden_count), BF16),
+        pltpu.VMEM((tokens, hidden_count), BF16),
+        pltpu.VMEM((features, tokens), BF16),
+        pltpu.VMEM((features, tokens), BF16),
+        dma((micro_count,)),
+        dma((micro_count,)),
+        dma((micro_count,)),
+        dma((micro_count,)),
+    ]
+    if inside:
+        up_rows, down_rows = features // shard_count, hidden_count // shard_count
+        scratch += [
+            pltpu.VMEM((features, hidden_count), BF16),
+            pltpu.VMEM((hidden_count, features), BF16),
+            pltpu.VMEM((shard_count, 8, features), F32),
+            pltpu.VMEM((shard_count, 8, features), F32),
+            pltpu.VMEM((8, features), F32),
+            pltpu.VMEM((chips, up_rows, hidden_count), BF16),
+            pltpu.VMEM((chips, down_rows, features), BF16),
+            pltpu.VMEM((chips + 1, up_rows, hidden_count), BF16),
+            pltpu.VMEM((chips + 1, down_rows, features), BF16),
+            dma((4, 2, chips)),
+            dma((4, chips)),
+            dma((4, chips)),
+            dma((4, chips)),
+            dma((2, chips)),
+            dma((2, chips + 1)),
+            dma((2, chips)),
+            dma((2, chips)),
+        ]
+        grads = (
+            jax.ShapeDtypeStruct((up_rows, hidden_count), F32),
+            jax.ShapeDtypeStruct((down_rows, features), F32),
+        )
+    else:
+        grads = (
             jax.ShapeDtypeStruct((features, hidden_count), BF16),
             jax.ShapeDtypeStruct((hidden_count, features), BF16),
-            jax.ShapeDtypeStruct((1, features), F32),
-        ),
+        )
+    return pl.pallas_call(
+        functools.partial(pipeline_kernel, section_count, shard_count),
+        out_shape=grads + (jax.ShapeDtypeStruct((8, features), F32),),
         in_specs=[vmem] * 9,
         out_specs=(vmem, vmem, vmem),
-        scratch_shapes=[
-            pltpu.VMEM(token, BF16),
-            pltpu.VMEM(token, BF16),
-            pltpu.VMEM(token, BF16),
-            pltpu.VMEM(token, BF16),
-            pltpu.VMEM((tokens, hidden_count), BF16),
-            pltpu.VMEM((tokens, hidden_count), BF16),
-            pltpu.VMEM((features, tokens), BF16),
-            pltpu.VMEM((features, tokens), BF16),
-            pltpu.SemaphoreType.DMA((micro_count,)),
-            pltpu.SemaphoreType.DMA((micro_count,)),
-            pltpu.SemaphoreType.DMA((micro_count,)),
-            pltpu.SemaphoreType.DMA((micro_count,)),
-        ],
+        scratch_shapes=scratch,
         compiler_params=pltpu.CompilerParams(
             collective_id=0, has_side_effects=True, vmem_limit_bytes=VMEM_BYTES
         ),
@@ -257,8 +548,12 @@
 
 def per_device(patches, cotangent, embed_blocks, ratio_index, depth, w_up, w_down, ln_gain):
     section_index = lax.axis_index("section")
+    shard_index = lax.axis_index("fsdp")
+    shard_count = lax.axis_size("fsdp")
     micro_count, rows, features = patches.shape
     hidden_count = w_up.shape[2]
+    gain_count = ln_gain.shape[1]
+    tiled = gain_count % 16 == 0 and w_down.shape[1] % 128 == 0 and shard_count % 2 == 0
 
     width = embed_blocks * BLOCK
     hidden_width = width * (6 + ratio_index) // 2
@@ -267,25 +562,29 @@
     active = (section_index < depth).astype(F32)
     live = embed * active[:, None]
     width_inv = jnp.broadcast_to((1.0 / width.astype(F32))[:, None, None], (micro_count, 1, BLOCK))
+    masks = (embed[:, None, :], live[:, None, :], hidden_mask[:, None, :], width_inv)
+    start = shard_index * gain_count
+
+    if tiled:
+        gain = jnp.zeros((8, features), F32)
+        gain = lax.dynamic_update_slice(gain, ln_gain.astype(F32), (jnp.int32(0), start))
+        own_up, own_down, gains = run_pipeline(
+            True, patches, cotangent, *masks, gain, w_up[0], w_down[0]
+        )
+        own_gain = lax.dynamic_slice(jnp.sum(gains, axis=0), (start,), (gain_count,))
+        return (own_up[None], own_down[None], own_gain[None])
 
     full_up = lax.all_gather(w_up[0], "fsdp", axis=0, tiled=True)
     full_down = lax.all_gather(w_down[0], "fsdp", axis=0, tiled=True)
     gain = lax.all_gather(ln_gain[0], "fsdp", axis=0, tiled=True).astype(F32)
-
-    part_up, part_down, part_gain = run_pipeline(
-        patches,
-        cotangent,
-        embed[:, None, :],
-        live[:, None, :],
-        hidden_mask[:, None, :],
-        width_inv,
-        gain[None],
-        full_up,
-        full_down,
+    gain = jnp.broadcast_to(gain[None], (8, features))
+    part_up, part_down, gains = run_pipeline(
+        False, patches, cotangent, *masks, gain, full_up, full_down
     )
     own_down = lax.psum_scatter(part_down, "fsdp", scatter_dimension=0, tiled=True)
     own_up = lax.psum_scatter(part_up, "fsdp", scatter_dimension=0, tiled=True)
-    own_gain = lax.psum_scatter(part_gain[0], "fsdp", scatter_dimension=0, tiled=True)
+    part_gain = jnp.sum(gains, axis=0)
+    own_gain = lax.psum_scatter(part_gain, "fsdp", scatter_dimension=0, tiled=True)
     return (own_up.astype(F32)[None], own_down.astype(F32)[None], own_gain[None])
 
 

time: 372 us -> 311 us (0.84)
  waiting for transfers between devices: 172 us -> 0 us
  Pallas kernels: 139 us -> 298 us
  blocking collectives: 33.1 us -> 0 us
  between operations: 15.1 us -> 0.65 us
    pallas_call x1, Pallas kernels: 139 us -> 298 us  [run_pipeline(): pl.pallas_call(functools.partial(pipeline_kernel, section_count, shard_co...]
    reduce_scatter x2 -> x0, waiting for transfers between devices: 89.3 us -> none  [the longest x1 53.1 us: per_device(): own_up = lax.psum_scatter(part_up, 'fsdp', scatter_dimension=0, tiled=True)]
    all_gather x2 -> x0, waiting for transfers between devices: 80.5 us -> none  [the longest x1 51.6 us: per_device(): full_down = lax.all_gather(w_down[0], 'fsdp', axis=0, tiled=True)]
    unnamed x2 -> x0, blocking collectives: 33.1 us -> none
    broadcast_in_dim x2 -> x0, other arithmetic: 4.33 us -> none  [the longest x1 2.18 us: per_device(): own_up.astype(F32)[None]]
  transfers between devices with their start and end apart: 4 -> 0, of which waited for: 4 -> 0; matrix products, arithmetic and copies ran while one was open for 3% -> 0% of each run, Pallas kernels for 0% -> 0%
where the time goes in v2:
time: 311 us; the launch traced here: 310 us
  Pallas kernels  298 us (96%)
  local copies, waits for them, and re-layouts  6.64 us (2%)
  other arithmetic  5.55 us (2%)
    pallas_call x1, Pallas kernels, run_pipeline(): pl.pallas_call(functools.partial(pipeline_kernel, section_count, shard_co...  298 us

profile of v2, /device:TPU:0, one launch (start us, length us, event | category | flops | bytes accessed | tf_op | source)
XLA Modules:
  0.0 310.4 jit_solution(7084050061582258394)
XLA Ops:
  0.6 0.7 convert_element_type.33
  1.3 0.6 broadcast_in_dim.11
  1.9 1.3 dynamic_update_slice.3.own_gain
  3.2 0.7 and_select_fusion
  3.9 0.7 compare_convert_fusion.2
  4.5 0.7 compare_select_fusion.live
  5.2 0.7 compare_convert_fusion.1.embed
  5.9 0.8 compare_convert_fusion.hidden_mask
  6.7 0.7 convert_divide_fusion
  7.3 0.7 broadcast_in_dim.10.width_inv
  8.0 297.5 %shard_map.103 = (f32[96,3072]{1,0:T(8,128)}, f32[384,768]{1,0:T(8,128)}, f32[8,768]{1,0:T(8,128)}) custom-call(bf16[8,128,768]{2,1,0:T(8,128)(2,1)} %patches.1, bf16[8,128,768]{2,1,0:T(8,128)(2,1)} %cotangent.1, f32[8,1,768]{2,1,0:T(1,128)} %compare_convert_fusion.1.embed, f32[8,1,768]{2,1,0:T(1,128)} %compare_select_fusion.live, ...), custom_call_target="tpu_custom_call" | custom-call | tf_op jit(solution)/shard_map/pallas_call | solution.py:537
  305.5 0.8 reduce_sum.9
  306.3 0.6 dynamic-slice_bitcast_fusion
  306.9 0.0 copy-start
  306.9 2.5 copy.14
  309.3 0.0 copy-done
  309.3 1.0 copy.15
Async XLA Ops:
  306.9 2.5 copy-start

commit v3 on v1

--- a/solution.py
+++ b/solution.py
@@ -1,4 +1,5 @@
 import functools
+import math
 
 import jax
 import jax.numpy as jnp
@@ -33,17 +34,22 @@
     return [(start, size) for start in range(0, total, size)]
 
 
+def signal(semaphore, device):
+    pl.semaphore_signal(semaphore, inc=1, device_id=device, device_id_type=MESH)
+
+
 def pipeline_kernel(
     section_count,
+    shard_count,
     patches,
     cotangent,
     embed,
     live,
     hidden_mask,
     width_inv,
-    gain_ref,
-    w_up,
-    w_down,
+    own_gain,
+    own_up,
+    own_down,
     grad_up,
     grad_down,
     grad_gain,
@@ -59,25 +65,329 @@
     fwd_recv,
     bwd_send,
     bwd_recv,
+    w_up=None,
+    w_down=None,
+    hold_up=None,
+    hold_down=None,
+    all_gain=None,
+    all_rise=None,
+    acc_gain=None,
+    pair_up=None,
+    pair_down=None,
+    first_up=None,
+    first_down=None,
+    second_up=None,
+    second_down=None,
+    plane_up=None,
+    plane_down=None,
+    last_up=None,
+    last_down=None,
+    token_send=None,
+    token_recv=None,
+    gain_send=None,
+    gain_recv=None,
+    scatter_send=None,
+    scatter_recv=None,
+    climb_send=None,
+    climb_recv=None,
+    side_send=None,
+    side_recv=None,
+    pair_send=None,
+    pair_recv=None,
+    sum_pair_send=None,
+    sum_pair_recv=None,
+    first_send=None,
+    first_recv=None,
+    second_send=None,
+    second_recv=None,
+    plane_send=None,
+    plane_recv=None,
+    last_send=None,
+    last_recv=None,
 ):
-    me = lax.axis_index("section")
+    planes = w_up is not None
+    column = lax.axis_index("section")
+    shard = lax.axis_index("fsdp")
+    chip = shard // 2
+    core = shard % 2
+    chips = shard_count // 2
+    me = chip if planes else column
+    stages = chips if planes else section_count
     is_first = me == 0
-    is_last = me == section_count - 1
+    is_last = me == stages - 1
     micro_count, rows, features = patches.shape
-    hidden_count = w_up.shape[1]
+    hidden_count = hidden_mask.shape[2]
+
+    def stage_device(stage):
+        return {"fsdp": 2 * stage + core} if planes else {"section": stage}
 
     barrier = pltpu.get_barrier_semaphore()
-
-    @pl.when(jnp.logical_not(is_first))
-    def _():
-        pl.semaphore_signal(barrier, inc=1, device_id={"section": me - 1}, device_id_type=MESH)
-
-    @pl.when(jnp.logical_not(is_last))
-    def _():
-        pl.semaphore_signal(barrier, inc=1, device_id={"section": me + 1}, device_id_type=MESH)
-
-    ends = is_first.astype(jnp.int32) + is_last.astype(jnp.int32)
-    pl.semaphore_wait(barrier, 2 - ends)
+    if planes:
+        for column_to in range(section_count):
+            for shard_to in range(shard_count):
+
+                @pl.when(jnp.logical_or(column != column_to, shard != shard_to))
+                def _():
+                    signal(barrier, {"section": column_to, "fsdp": shard_to})
+
+        pl.semaphore_wait(barrier, section_count * shard_count - 1)
+    else:
+
+        @pl.when(jnp.logical_not(is_first))
+        def _():
+            signal(barrier, {"section": me - 1})
+
+        @pl.when(jnp.logical_not(is_last))
+        def _():
+            signal(barrier, {"section": me + 1})
+
+        pl.semaphore_wait(barrier, 2 - is_first.astype(jnp.int32) - is_last.astype(jnp.int32))
+
+    def remote(source, target, send, recv, device):
+        return pltpu.make_async_remote_copy(
+            src_ref=source,
+            dst_ref=target,
+            send_sem=send,
+            recv_sem=recv,
+            device_id=device,
+            device_id_type=MESH,
+        )
+
+    if planes:
+        beside = column + 1 - 2 * (column % 2)
+        across = column + 2 - 4 * (column // 2)
+        corner = 3 - column
+        near = (column, beside, across, corner)
+        other = {"fsdp": shard + 1 - 2 * core}
+        up_rows, down_rows = features // shard_count, hidden_count // shard_count
+        up_cols, down_part = hidden_count // section_count, down_rows // section_count
+        share = rows // section_count
+
+        def at_rows(start, size):
+            return pl.ds(pl.multiple_of(start, size), size)
+
+        def piece(number, full, place, which):
+            if number == 0:
+                return full.at[at_rows((2 * place + core) * up_rows, up_rows), at_rows(which * up_cols, up_cols)]
+            return full.at[at_rows(((2 * place + core) * section_count + which) * down_part, down_part), :]
+
+        def own_piece(number, which):
+            if number == 0:
+                return own_up.at[:, at_rows(which * up_cols, up_cols)]
+            return own_down.at[at_rows(which * down_part, down_part), :]
+
+        fulls = (w_up, w_down)
+        holds = (hold_up, hold_down)
+
+        def token_copy(number, m, source):
+            raw, land, stage = ((patches, x_in, 0), (cotangent, g_in, stages - 1))[number]
+            return remote(
+                raw.at[m, at_rows(column * share, share), :],
+                land.at[m, at_rows(source * share, share), :],
+                token_send.at[number, m],
+                token_recv.at[number, m, source],
+                stage_device(stage),
+            )
+
+        def send_tokens(number, first, last):
+            raw, land, stage = ((patches, x_in, 0), (cotangent, g_in, stages - 1))[number]
+
+            @pl.when(chip != stage)
+            def _():
+                for m in range(first, last):
+                    token_copy(number, m, chip).start()
+
+            @pl.when(chip == stage)
+            def _():
+                for m in range(first, last):
+                    land[m, at_rows(chip * share, share), :] = raw[m, at_rows(column * share, share), :]
+
+        def wait_tokens(number, m):
+            for source in range(chips):
+
+                @pl.when(chip != source)
+                def _():
+                    token_copy(number, m, source).wait_recv()
+
+        def scatter_copy(number, far):
+            return remote(
+                own_piece(number, near[far]),
+                holds[number].at[column],
+                scatter_send.at[number, far - 1],
+                scatter_recv.at[number, column],
+                {"section": near[far]},
+            )
+
+        def scatter_wait(number, source):
+            hold = holds[number]
+            remote(
+                hold.at[source],
+                hold.at[source],
+                scatter_send.at[number, 0],
+                scatter_recv.at[number, source],
+                {"section": beside},
+            ).wait_recv()
+
+        def climb_copy(number, source, layer, place):
+            return remote(
+                source,
+                piece(number, fulls[number], place, column),
+                climb_send.at[number, layer],
+                climb_recv.at[number, place],
+                {"fsdp": 2 * layer + core},
+            )
+
+        def side_copy(number, way, place, which, kind, device):
+            spot = piece(number, fulls[number], place, which)
+            return remote(
+                spot,
+                spot,
+                side_send.at[number, way, place],
+                side_recv.at[number, kind, place],
+                {"section": device},
+            )
+
+        def to_beside(number, place):
+            return side_copy(number, 0, place, column, 0, beside)
+
+        def to_across(number, place):
+            return side_copy(number, 1, place, column, 1, across)
+
+        def relay(number, place):
+            if number == 0:
+                return side_copy(number, 2, place, beside, 2, across)
+            return side_copy(number, 2, place, across, 2, beside)
+
+        def arrived(number, place, kind):
+            side_copy(number, 0, place, near[kind + 1], kind, beside).wait_recv()
+
+        def pair_copy(number, place, far, parity):
+            which = near[far]
+            full = fulls[number]
+            if number == 0:
+                spot = full.at[at_rows((2 * place + parity) * up_rows, up_rows), at_rows(which * up_cols, up_cols)]
+            else:
+                first = ((2 * place + parity) * section_count + which) * down_part
+                spot = full.at[at_rows(first, down_part), :]
+            return remote(
+                spot, spot, pair_send.at[number, far, place], pair_recv.at[number, far, place], other
+            )
+
+        def gain_targets(number):
+            if number == 0:
+                return [(j, 2 * column + half, 2 * j + half) for j in range(section_count) for half in range(2)]
+            return [(chip, place, place) for place in range(shard_count)]
+
+        def open_gain(block, land, number):
+            source = shard if number == 0 else 2 * column + core
+            for column_to, shard_to, index in gain_targets(number):
+                copy = remote(
+                    block,
+                    land.at[source],
+                    gain_send.at[number, index],
+                    gain_recv.at[number, source],
+                    {"section": column_to, "fsdp": shard_to},
+                )
+
+                @pl.when(jnp.logical_or(column_to != column, shard_to != shard))
+                def _():
+                    copy.start()
+
+            @pl.when(chip == column)
+            def _():
+                land[source] = block[...]
+
+        def close_gain(block, land, number):
+            mine = shard if number == 0 else 2 * column + core
+            for source in range(shard_count):
+
+                @pl.when(jnp.logical_or(chip != column, source != mine))
+                def _():
+                    remote(
+                        block, land.at[source], gain_send.at[number, 0], gain_recv.at[number, source], other
+                    ).wait_recv()
+
+        def sent_gain(block, land, number):
+            for column_to, shard_to, index in gain_targets(number):
+
+                @pl.when(jnp.logical_or(column_to != column, shard_to != shard))
+                def _():
+                    remote(
+                        block, land.at[0], gain_send.at[number, index], gain_recv.at[number, 0], other
+                    ).wait_send()
+
+        both = (0, 1)
+        for number in both:
+            for far in (1, 2, 3):
+                scatter_copy(number, far).start()
+        send_tokens(0, 0, 1)
+        open_gain(own_gain, all_gain, 0)
+        for far in (0, 1, 2, 3):
+            layer = near[far]
+            for number in both:
+                if far == 0:
+                    source = own_piece(number, column)
+                else:
+                    scatter_wait(number, layer)
+                    source = holds[number].at[layer]
+
+                @pl.when(layer != chip)
+                def _():
+                    climb_copy(number, source, layer, chip).start()
+
+                @pl.when(layer == chip)
+                def _():
+                    spot = piece(number, fulls[number], chip, column)
+                    spot[...] = source[...]
+
+        send_tokens(0, 1, micro_count)
+        send_tokens(1, 0, micro_count)
+
+        def own_turn(step):
+            place = lax.rem(chip + step, chips)
+            for number in both:
+                if step > 0:
+                    spot = piece(number, fulls[number], place, column)
+                    climb_copy(number, spot, chip, place).wait_recv()
+                to_beside(number, place).start()
+                to_across(number, place).start()
+                pair_copy(number, place, 0, core).start()
+
+        def side_turn(step):
+            place = lax.rem(chip + step, chips)
+            arrived(0, place, 0)
+            relay(0, place).start()
+            pair_copy(0, place, 1, core).start()
+            arrived(1, place, 1)
+            relay(1, place).start()
+            pair_copy(1, place, 2, core).start()
+            arrived(0, place, 1)
+            pair_copy(0, place, 2, core).start()
+            arrived(1, place, 0)
+            pair_copy(1, place, 1, core).start()
+
+        def corner_turn(step):
+            place = lax.rem(chip + step, chips)
+            for number in both:
+                arrived(number, place, 2)
+                pair_copy(number, place, 3, core).start()
+
+        for step in range(chips + 2):
+            if step < chips:
+                own_turn(step)
+            if 1 <= step <= chips:
+                side_turn(step - 1)
+            if 2 <= step:
+                corner_turn(step - 2)
+        for place in range(chips):
+            for far in (0, 1, 2, 3):
+                for number in both:
+                    pair_copy(number, place, far, 1 - core).wait_recv()
+        close_gain(own_gain, all_gain, 0)
+        gain = jnp.sum(all_gain[...], axis=0)[:1]
+    else:
+        w_up, w_down, acc_gain = own_up, own_down, grad_gain
+        gain = own_gain[:1]
 
     def forward_copy(m):
         return pltpu.make_async_remote_copy(
@@ -85,7 +395,7 @@
             dst_ref=x_in.at[m],
             send_sem=fwd_send.at[m],
             recv_sem=fwd_recv.at[m],
-            device_id={"section": jnp.minimum(me + 1, section_count - 1)},
+            device_id=stage_device(jnp.minimum(me + 1, stages - 1)),
             device_id_type=MESH,
         )
 
@@ -95,7 +405,7 @@
             dst_ref=g_in.at[m],
             send_sem=bwd_send.at[m],
             recv_sem=bwd_recv.at[m],
-            device_id={"section": jnp.maximum(me - 1, 0)},
+            device_id=stage_device(jnp.maximum(me - 1, 0)),
             device_id_type=MESH,
         )
 
@@ -109,14 +419,16 @@
         inv_std = lax.rsqrt(variance + EPSILON)
         return centered * inv_std, inv_std
 
-    gain = gain_ref[...]
-
     def forward(m, carry):
         at = pl.ds(pl.multiple_of(m * rows, rows), rows)
 
         @pl.when(is_first)
         def _():
-            x_in[m] = (patches[m].astype(F32) * embed[m]).astype(BF16)
+            if planes:
+                wait_tokens(0, m)
+                x_in[m] = (x_in[m].astype(F32) * embed[m]).astype(BF16)
+            else:
+                x_in[m] = (patches[m].astype(F32) * embed[m]).astype(BF16)
 
         @pl.when(jnp.logical_not(is_first))
         def _():
@@ -146,14 +458,18 @@
         return carry
 
     lax.fori_loop(0, micro_count, forward, 0)
-    grad_gain[...] = jnp.zeros_like(grad_gain)
+    acc_gain[...] = jnp.zeros_like(acc_gain)
 
     def backward(m, carry):
         at = pl.ds(pl.multiple_of(m * rows, rows), rows)
 
         @pl.when(is_last)
         def _():
-            g_in[m] = (cotangent[m].astype(F32) * embed[m]).astype(BF16)
+            if planes:
+                wait_tokens(1, m)
+                g_in[m] = (g_in[m].astype(F32) * embed[m]).astype(BF16)
+            else:
+                g_in[m] = (cotangent[m].astype(F32) * embed[m]).astype(BF16)
 
         @pl.when(jnp.logical_not(is_last))
         def _():
@@ -178,7 +494,7 @@
         standard, inv_std = layer_norm(m)
         mask = embed[m]
         scale = width_inv[m][:, :1]
-        grad_gain[...] += jnp.sum(grad_normed * standard, axis=0, keepdims=True)
+        acc_gain[...] += jnp.sum((grad_normed * standard).reshape(-1, 8, features), axis=0)
 
         @pl.when(jnp.logical_not(is_first))
         def _():
@@ -195,15 +511,223 @@
 
     width = 256 if hidden_count % 256 == 0 else hidden_count
 
+    def up_grads(first, size, step):
+        part = pl.ds(pl.multiple_of(step * width, width), width)
+        these = pl.ds(first, size)
+        return these, part, jnp.dot(normed_t[these, :], slope[:, part], preferred_element_type=F32)
+
+    def down_grads(part):
+        down = jnp.dot(branch_t[...], act[:, part], preferred_element_type=F32)
+        return jnp.transpose(down).astype(BF16)
+
     def weight_grads(step, carry):
-        part = pl.ds(pl.multiple_of(step * width, width), width)
-        up = jnp.dot(normed_t[...], slope[:, part], preferred_element_type=F32)
-        grad_up[:, part] = up.astype(BF16)
-        down = jnp.dot(branch_t[...], act[:, part], preferred_element_type=F32)
-        grad_down[part, :] = jnp.transpose(down).astype(BF16)
+        these, part, up = up_grads(0, features, step)
+        grad_up[these, part] = up.astype(BF16)
+        grad_down[part, :] = down_grads(part)
         return carry
 
-    lax.fori_loop(0, hidden_count // width, weight_grads, 0)
+    def slot(full, index):
+        size = full.shape[0] // shard_count
+        return full.at[pl.ds(pl.multiple_of(index * size, size), size)]
+
+    if planes:
+        pairs = (pair_up, pair_down)
+        firsts = (first_up, first_down)
+        seconds = (second_up, second_down)
+        finals = (plane_up, plane_down)
+        lasts = (last_up, last_down)
+        first_way = (beside, across)
+        second_way = (across, beside)
+        kept = (across, beside)
+
+        def sum_pair(number, place):
+            return remote(
+                slot(fulls[number], 2 * place + 1 - core),
+                pairs[number].at[place],
+                sum_pair_send.at[number, place],
+                sum_pair_recv.at[number, place],
+                other,
+            )
+
+        def first_copy(number, place, index):
+            which = (first_way[number], corner)[index]
+            return remote(
+                piece(number, fulls[number], place, which),
+                firsts[number].at[place, index],
+                first_send.at[number, place, index],
+                first_recv.at[number, place, index],
+                {"section": first_way[number]},
+            )
+
+        def second_copy(number, place):
+            return remote(
+                piece(number, fulls[number], place, kept[number]),
+                seconds[number].at[place],
+                second_send.at[number, place],
+                second_recv.at[number, place],
+                {"section": second_way[number]},
+            )
+
+        def plane_copy(number, place, layer):
+            return remote(
+                piece(number, fulls[number], place, column),
+                finals[number].at[layer],
+                plane_send.at[number, place],
+                plane_recv.at[number, layer],
+                {"fsdp": 2 * place + core},
+            )
+
+        def last_copy(number, layer, source):
+            return remote(
+                finals[number].at[layer],
+                lasts[number].at[source],
+                last_send.at[number, layer],
+                last_recv.at[number, source],
+                {"section": layer},
+            )
+
+        def make_grads(place):
+            up_size = 2 * up_rows
+            first_row = pl.multiple_of(place * up_size, up_size)
+
+            def up_step(step, carry):
+                these, part, up = up_grads(first_row, up_size, step)
+                w_up[these, part] = up.astype(BF16)
+                return carry
+
+            lax.fori_loop(0, hidden_count // width, up_step, 0)
+            sum_pair(0, place).start()
+            down_size = 2 * down_rows
+            size = math.gcd(down_size, width)
+
+            def down_step(step, carry):
+                part = at_rows(place * down_size + step * size, size)
+                w_down[part, :] = down_grads(part)
+                return carry
+
+            lax.fori_loop(0, down_size // size, down_step, 0)
+            sum_pair(1, place).start()
+
+        def first_turn(place):
+            for number in both:
+                mine = slot(fulls[number], 2 * place + core)
+                sum_pair(number, place).wait_recv()
+                mine[...] = (mine[...].astype(F32) + pairs[number][place].astype(F32)).astype(BF16)
+                for index in (0, 1):
+                    first_copy(number, place, index).start()
+
+        def second_turn(place):
+            for number in both:
+                for index in (1, 0):
+                    first_copy(number, place, index).wait_recv()
+                spot = piece(number, fulls[number], place, kept[number])
+                total = spot[...].astype(F32) + firsts[number][place, 1].astype(F32)
+                spot[...] = total.astype(BF16)
+                second_copy(number, place).start()
+
+        def plane_turn(place):
+            for number in both:
+                second_copy(number, place).wait_recv()
+                spot = piece(number, fulls[number], place, column)
+                total = spot[...].astype(F32) + firsts[number][place, 0].astype(F32)
+                total = (total + seconds[number][place].astype(F32)).astype(BF16)
+
+                @pl.when(place != chip)
+                def _():
+                    spot[...] = total
+                    plane_copy(number, place, chip).start()
+
+                @pl.when(place == chip)
+                def _():
+                    finals[number][chip] = total
+
+        def place_at(index):
+            return lax.rem(chip + chips - 1 - index + chips, chips)
+
+        def reduce_step(index, carry):
+            @pl.when(index < chips)
+            def _():
+                make_grads(place_at(index))
+                first_turn(place_at(index))
+
+            @pl.when(jnp.logical_and(index >= 1, index <= chips))
+            def _():
+                second_turn(place_at(jnp.maximum(index - 1, 0)))
+
+            @pl.when(index >= 2)
+            def _():
+                plane_turn(place_at(jnp.maximum(index - 2, 0)))
+
+            return carry
+
+        open_gain(acc_gain, all_rise, 1)
+        for number in both:
+            for far in (1, 2, 3):
+                scatter_copy(number, far).wait_send()
+            for layer in range(chips):
+
+                @pl.when(chip != layer)
+                def _():
+                    climb_copy(number, holds[number].at[layer], layer, chip).wait_send()
+
+            for place in range(chips):
+                to_beside(number, place).wait_send()
+                to_across(number, place).wait_send()
+                relay(number, place).wait_send()
+                for far in (0, 1, 2, 3):
+                    pair_copy(number, place, far, core).wait_send()
+        sent_gain(own_gain, all_gain, 0)
+        lax.fori_loop(0, chips + 2, reduce_step, 0)
+        for layer in reversed(range(chips)):
+            for number in both:
+
+                @pl.when(layer != chip)
+                def _():
+                    plane_copy(number, chip, layer).wait_recv()
+
+                @pl.when(layer != column)
+                def _():
+                    last_copy(number, layer, column).start()
+
+                @pl.when(layer == column)
+                def _():
+                    lasts[number][layer] = finals[number][layer]
+
+        close_gain(acc_gain, all_rise, 1)
+        grad_gain[...] = jnp.sum(all_rise[...], axis=0)
+        for source in range(section_count):
+            for number in both:
+
+                @pl.when(source != column)
+                def _():
+                    last_copy(number, source, source).wait_recv()
+
+            grad_up[:, pl.ds(source * up_cols, up_cols)] = last_up[source].astype(F32)
+            grad_down[pl.ds(source * down_part, down_part), :] = last_down[source].astype(F32)
+        sent_gain(acc_gain, all_rise, 1)
+        for number in both:
+            for place in range(chips):
+                sum_pair(number, place).wait_send()
+                second_copy(number, place).wait_send()
+                for index in (0, 1):
+                    first_copy(number, place, index).wait_send()
+
+                @pl.when(place != chip)
+                def _():
+                    plane_copy(number, place, chip).wait_send()
+
+                @pl.when(place != column)
+                def _():
+                    last_copy(number, place, column).wait_send()
+
+        for number, stage in ((0, 0), (1, stages - 1)):
+
+            @pl.when(chip != stage)
+            def _():
+                for m in range(micro_count):
+                    token_copy(number, m, chip).wait_send()
+    else:
+        lax.fori_loop(0, hidden_count // width, weight_grads, 0)
 
     def drain(m, carry):
         @pl.when(jnp.logical_not(is_last))
@@ -219,36 +743,90 @@
     lax.fori_loop(0, micro_count, drain, 0)
 
 
-def run_pipeline(patches, cotangent, embed, live, hidden_mask, width_inv, gain, w_up, w_down):
+def run_pipeline(planes, patches, cotangent, embed, live, hidden_mask, width_inv, gain, w_up, w_down):
     section_count = lax.axis_size("section")
+    shard_count = lax.axis_size("fsdp")
     micro_count, rows, features = patches.shape
     hidden_count = w_up.shape[1]
     vmem = pl.BlockSpec(memory_space=pltpu.VMEM)
     token = (micro_count, rows, features)
     tokens = micro_count * rows
-    return pl.pallas_call(
-        functools.partial(pipeline_kernel, section_count),
-        out_shape=(
+    chips = shard_count // 2
+    dma = pltpu.SemaphoreType.DMA
+    scratch = [
+        pltpu.VMEM(token, BF16),
+        pltpu.VMEM(token, BF16),
+        pltpu.VMEM(token, BF16),
+        pltpu.VMEM(token, BF16),
+        pltpu.VMEM((tokens, hidden_count), BF16),
+        pltpu.VMEM((tokens, hidden_count), BF16),
+        pltpu.VMEM((features, tokens), BF16),
+        pltpu.VMEM((features, tokens), BF16),
+        dma((micro_count,)),
+        dma((micro_count,)),
+        dma((micro_count,)),
+        dma((micro_count,)),
+    ]
+    if planes:
+        up_rows, down_rows = features // shard_count, hidden_count // shard_count
+        up_piece = (up_rows, hidden_count // section_count)
+        down_piece = (down_rows // section_count, features)
+        scratch += [
+            pltpu.VMEM((features, hidden_count), BF16),
+            pltpu.VMEM((hidden_count, features), BF16),
+            pltpu.VMEM((section_count,) + up_piece, BF16),
+            pltpu.VMEM((section_count,) + down_piece, BF16),
+            pltpu.VMEM((shard_count, 8, features), F32),
+            pltpu.VMEM((shard_count, 8, features), F32),
+            pltpu.VMEM((8, features), F32),
+            pltpu.VMEM((chips, up_rows, hidden_count), BF16),
+            pltpu.VMEM((chips, down_rows, features), BF16),
+            pltpu.VMEM((chips, 2) + up_piece, BF16),
+            pltpu.VMEM((chips, 2) + down_piece, BF16),
+            pltpu.VMEM((chips,) + up_piece, BF16),
+            pltpu.VMEM((chips,) + down_piece, BF16),
+            pltpu.VMEM((chips,) + up_piece, BF16),
+            pltpu.VMEM((chips,) + down_piece, BF16),
+            pltpu.VMEM((section_count,) + up_piece, BF16),
+            pltpu.VMEM((section_count,) + down_piece, BF16),
+            dma((2, micro_count)),
+            dma((2, micro_count, chips)),
+            dma((2, shard_count)),
+            dma((2, shard_count)),
+            dma((2, 3)),
+            dma((2, section_count)),
+            dma((2, chips)),
+            dma((2, chips)),
+            dma((2, 3, chips)),
+            dma((2, 3, chips)),
+            dma((2, 4, chips)),
+            dma((2, 4, chips)),
+            dma((2, chips)),
+            dma((2, chips)),
+            dma((2, chips, 2)),
+            dma((2, chips, 2)),
+            dma((2, chips)),
+            dma((2, chips)),
+            dma((2, chips)),
+            dma((2, chips)),
+            dma((2, chips)),
+            dma((2, section_count)),
+        ]
+        grads = (
+            jax.ShapeDtypeStruct((up_rows, hidden_count), F32),
+            jax.ShapeDtypeStruct((down_rows, features), F32),
+        )
+    else:
+        grads = (
             jax.ShapeDtypeStruct((features, hidden_count), BF16),
             jax.ShapeDtypeStruct((hidden_count, features), BF16),
-            jax.ShapeDtypeStruct((1, features), F32),
-        ),
+        )
+    return pl.pallas_call(
+        functools.partial(pipeline_kernel, section_count, shard_count),
+        out_shape=grads + (jax.ShapeDtypeStruct((8, features), F32),),
         in_specs=[vmem] * 9,
         out_specs=(vmem, vmem, vmem),
-        scratch_shapes=[
-            pltpu.VMEM(token, BF16),
-            pltpu.VMEM(token, BF16),
-            pltpu.VMEM(token, BF16),
-            pltpu.VMEM(token, BF16),
-            pltpu.VMEM((tokens, hidden_count), BF16),
-            pltpu.VMEM((tokens, hidden_count), BF16),
-            pltpu.VMEM((features, tokens), BF16),
-            pltpu.VMEM((features, tokens), BF16),
-            pltpu.SemaphoreType.DMA((micro_count,)),
-            pltpu.SemaphoreType.DMA((micro_count,)),
-            pltpu.SemaphoreType.DMA((micro_count,)),
-            pltpu.SemaphoreType.DMA((micro_count,)),
-        ],
+        scratch_shapes=scratch,
         compiler_params=pltpu.CompilerParams(
             collective_id=0, has_side_effects=True, vmem_limit_bytes=VMEM_BYTES
         ),
@@ -257,35 +835,53 @@
 
 def per_device(patches, cotangent, embed_blocks, ratio_index, depth, w_up, w_down, ln_gain):
     section_index = lax.axis_index("section")
+    shard_index = lax.axis_index("fsdp")
+    shard_count = lax.axis_size("fsdp")
     micro_count, rows, features = patches.shape
     hidden_count = w_up.shape[2]
+    gain_count = ln_gain.shape[1]
+    section_count = lax.axis_size("section")
+    down_part = w_down.shape[1] // section_count
+    planes = (
+        section_count == 4
+        and shard_count == 2 * section_count
+        and gain_count % 16 == 0
+        and down_part % 16 == 0
+        and hidden_count % (128 * section_count) == 0
+        and rows % (16 * section_count) == 0
+    )
 
     width = embed_blocks * BLOCK
     hidden_width = width * (6 + ratio_index) // 2
     embed = (lax.iota(jnp.int32, features)[None, :] < width[:, None]).astype(F32)
     hidden_mask = (lax.iota(jnp.int32, hidden_count)[None, :] < hidden_width[:, None]).astype(F32)
-    active = (section_index < depth).astype(F32)
+    layer = shard_index // 2 if planes else section_index
+    active = (layer < depth).astype(F32)
     live = embed * active[:, None]
     width_inv = jnp.broadcast_to((1.0 / width.astype(F32))[:, None, None], (micro_count, 1, BLOCK))
+    masks = (embed[:, None, :], live[:, None, :], hidden_mask[:, None, :], width_inv)
+    start = shard_index * gain_count
+
+    if planes:
+        gain = jnp.zeros((8, features), F32)
+        gain = lax.dynamic_update_slice(gain, ln_gain.astype(F32), (jnp.int32(0), start))
+        own_up, own_down, gains = run_pipeline(
+            True, patches, cotangent, *masks, gain, w_up[0], w_down[0]
+        )
+        own_gain = lax.dynamic_slice(jnp.sum(gains, axis=0), (start,), (gain_count,))
+        return (own_up[None], own_down[None], own_gain[None])
 
     full_up = lax.all_gather(w_up[0], "fsdp", axis=0, tiled=True)
     full_down = lax.all_gather(w_down[0], "fsdp", axis=0, tiled=True)
     gain = lax.all_gather(ln_gain[0], "fsdp", axis=0, tiled=True).astype(F32)
-
-    part_up, part_down, part_gain = run_pipeline(
-        patches,
-        cotangent,
-        embed[:, None, :],
-        live[:, None, :],
-        hidden_mask[:, None, :],
-        width_inv,
-        gain[None],
-        full_up,
-        full_down,
+    gain = jnp.broadcast_to(gain[None], (8, features))
+    part_up, part_down, gains = run_pipeline(
+        False, patches, cotangent, *masks, gain, full_up, full_down
     )
     own_down = lax.psum_scatter(part_down, "fsdp", scatter_dimension=0, tiled=True)
     own_up = lax.psum_scatter(part_up, "fsdp", scatter_dimension=0, tiled=True)
-    own_gain = lax.psum_scatter(part_gain[0], "fsdp", scatter_dimension=0, tiled=True)
+    part_gain = jnp.sum(gains, axis=0)
+    own_gain = lax.psum_scatter(part_gain, "fsdp", scatter_dimension=0, tiled=True)
     return (own_up.astype(F32)[None], own_down.astype(F32)[None], own_gain[None])
 
 

time: 372 us -> 286 us (0.77)
  waiting for transfers between devices: 172 us -> 0 us
  Pallas kernels: 139 us -> 273 us
  blocking collectives: 33.1 us -> 0 us
  between operations: 15.1 us -> 0.66 us
    pallas_call x1, Pallas kernels: 139 us -> 273 us  [run_pipeline(): pl.pallas_call(functools.partial(pipeline_kernel, section_count, shard_co...]
    reduce_scatter x2 -> x0, waiting for transfers between devices: 89.3 us -> none  [the longest x1 53.1 us: per_device(): own_up = lax.psum_scatter(part_up, 'fsdp', scatter_dimension=0, tiled=True)]
    all_gather x2 -> x0, waiting for transfers between devices: 80.5 us -> none  [the longest x1 51.6 us: per_device(): full_down = lax.all_gather(w_down[0], 'fsdp', axis=0, tiled=True)]
    unnamed x2 -> x0, blocking collectives: 33.1 us -> none
    broadcast_in_dim x2 -> x0, other arithmetic: 4.33 us -> none  [the longest x1 2.18 us: per_device(): own_up.astype(F32)[None]]
  transfers between devices with their start and end apart: 4 -> 0, of which waited for: 4 -> 0; matrix products, arithmetic and copies ran while one was open for 3% -> 0% of each run, Pallas kernels for 0% -> 0%
where the time goes in v3:
time: 286 us; the launch traced here: 285 us
  Pallas kernels  273 us (95%)
  local copies, waits for them, and re-layouts  6.63 us (2%)
  other arithmetic  5.55 us (2%)
    pallas_call x1, Pallas kernels, run_pipeline(): pl.pallas_call(functools.partial(pipeline_kernel, section_count, shard_co...  273 us

profile of v3, /device:TPU:0, one launch (start us, length us, event | category | flops | bytes accessed | tf_op | source)
XLA Modules:
  0.0 285.4 jit_solution(16538904375762253497)
XLA Ops:
  0.6 0.7 compare_convert_fusion.2
  1.3 0.7 convert_element_type.33
  2.0 0.7 convert_divide_fusion
  2.6 0.7 and_select_fusion
  3.3 0.7 broadcast_in_dim.10.width_inv
  4.0 0.7 compare_select_fusion.live
  4.7 0.7 compare_convert_fusion.1.embed
  5.4 0.6 broadcast_in_dim.11
  6.0 1.3 dynamic_update_slice.3.own_gain
  7.3 0.8 compare_convert_fusion.hidden_mask
  8.0 272.5 %shard_map.103 = (f32[96,3072]{1,0:T(8,128)}, f32[384,768]{1,0:T(8,128)}, f32[8,768]{1,0:T(8,128)}) custom-call(bf16[8,128,768]{2,1,0:T(8,128)(2,1)} %patches.1, bf16[8,128,768]{2,1,0:T(8,128)(2,1)} %cotangent.1, f32[8,1,768]{2,1,0:T(1,128)} %compare_convert_fusion.1.embed, f32[8,1,768]{2,1,0:T(1,128)} %compare_select_fusion.live, ...), custom_call_target="tpu_custom_call" | custom-call | tf_op jit(solution)/shard_map/pallas_call | solution.py:824
  280.5 0.8 reduce_sum.9
  281.3 0.6 dynamic-slice_bitcast_fusion
  281.9 0.0 copy-start
  281.9 2.5 copy.14
  284.3 0.0 copy-done
  284.4 1.0 copy.15
Async XLA Ops:
  281.9 2.5 copy-start

commit v4 on v3

--- a/solution.py
+++ b/solution.py
@@ -9,6 +9,7 @@
 from jax.sharding import PartitionSpec as P
 
 BLOCK = 128
+SPLIT = False
 EPSILON = 1e-05
 SCALE = 0.7978845608028654
 MESH = pl.DeviceIdType.MESH
@@ -43,10 +44,7 @@
     shard_count,
     patches,
     cotangent,
-    embed,
-    live,
-    hidden_mask,
-    width_inv,
+    table,
     own_gain,
     own_up,
     own_down,
@@ -71,6 +69,8 @@
     hold_down=None,
     all_gain=None,
     all_rise=None,
+    rise_own=None,
+    rise_sum=None,
     acc_gain=None,
     pair_up=None,
     pair_down=None,
@@ -86,6 +86,8 @@
     token_recv=None,
     gain_send=None,
     gain_recv=None,
+    rise_send=None,
+    rise_recv=None,
     scatter_send=None,
     scatter_recv=None,
     climb_send=None,
@@ -116,21 +118,32 @@
     is_first = me == 0
     is_last = me == stages - 1
     micro_count, rows, features = patches.shape
-    hidden_count = hidden_mask.shape[2]
+    hidden_count = table.shape[2]
+    features_all = pl.ds(0, features)
+    halves = micro_count // table.shape[0]
+
+    def hidden_mask(m, part):
+        return table[m // halves, 0:1, part]
+
+    def embed(m, part=features_all):
+        return table[m // halves, 1:2, part]
+
+    def live(m, part=features_all):
+        return table[m // halves, 2:3, part]
+
+    def width_inv(m):
+        return table[m // halves, 3:4, 0:1]
 
     def stage_device(stage):
         return {"fsdp": 2 * stage + core} if planes else {"section": stage}
 
     barrier = pltpu.get_barrier_semaphore()
     if planes:
-        for column_to in range(section_count):
-            for shard_to in range(shard_count):
-
-                @pl.when(jnp.logical_or(column != column_to, shard != shard_to))
-                def _():
-                    signal(barrier, {"section": column_to, "fsdp": shard_to})
-
-        pl.semaphore_wait(barrier, section_count * shard_count - 1)
+        for step in range(1, section_count):
+            signal(barrier, {"section": lax.rem(column + step, section_count)})
+            signal(barrier, {"fsdp": lax.rem(shard + 2 * step, shard_count)})
+        signal(barrier, {"fsdp": shard + 1 - 2 * core})
+        pl.semaphore_wait(barrier, 2 * section_count - 1)
     else:
 
         @pl.when(jnp.logical_not(is_first))
@@ -273,55 +286,61 @@
                 spot, spot, pair_send.at[number, far, place], pair_recv.at[number, far, place], other
             )
 
-        def gain_targets(number):
-            if number == 0:
-                return [(j, 2 * column + half, 2 * j + half) for j in range(section_count) for half in range(2)]
-            return [(chip, place, place) for place in range(shard_count)]
-
-        def open_gain(block, land, number):
-            source = shard if number == 0 else 2 * column + core
-            for column_to, shard_to, index in gain_targets(number):
-                copy = remote(
-                    block,
-                    land.at[source],
-                    gain_send.at[number, index],
-                    gain_recv.at[number, source],
-                    {"section": column_to, "fsdp": shard_to},
-                )
-
-                @pl.when(jnp.logical_or(column_to != column, shard_to != shard))
-                def _():
-                    copy.start()
-
-            @pl.when(chip == column)
+        is_hub = chip == column
+
+        def gain_copy(source, place, way, device):
+            return remote(
+                source,
+                all_gain.at[2 * place + core],
+                gain_send.at[way, place],
+                gain_recv.at[2 * place + core],
+                device,
+            )
+
+        def to_hub():
+            return gain_copy(own_gain, chip, 0, {"fsdp": 2 * column + core})
+
+        def from_hub(place, far):
+            device = other if far == 0 else {"section": near[far]}
+            return gain_copy(all_gain.at[2 * place + core], place, far + 1, device)
+
+        def wait_gain(index):
+            remote(
+                all_gain.at[index], all_gain.at[index], gain_send.at[0, 0], gain_recv.at[index], other
+            ).wait_recv()
+
+        def share_gain():
+            @pl.when(is_hub)
             def _():
-                land[source] = block[...]
-
-        def close_gain(block, land, number):
-            mine = shard if number == 0 else 2 * column + core
-            for source in range(shard_count):
-
-                @pl.when(jnp.logical_or(chip != column, source != mine))
-                def _():
-                    remote(
-                        block, land.at[source], gain_send.at[number, 0], gain_recv.at[number, source], other
-                    ).wait_recv()
-
-        def sent_gain(block, land, number):
-            for column_to, shard_to, index in gain_targets(number):
-
-                @pl.when(jnp.logical_or(column_to != column, shard_to != shard))
-                def _():
-                    remote(
-                        block, land.at[0], gain_send.at[number, index], gain_recv.at[number, 0], other
-                    ).wait_send()
+                for place in range(chips):
+
+                    @pl.when(place != chip)
+                    def _():
+                        wait_gain(2 * place + core)
+
+                    for far in (1, 2, 3, 0):
+                        from_hub(place, far).start()
+
+            @pl.when(jnp.logical_not(is_hub))
+            def _():
+                for place in range(chips):
+                    wait_gain(2 * place + core)
+                    from_hub(place, 0).start()
 
         both = (0, 1)
         for number in both:
             for far in (1, 2, 3):
                 scatter_copy(number, far).start()
         send_tokens(0, 0, 1)
-        open_gain(own_gain, all_gain, 0)
+
+        @pl.when(is_hub)
+        def _():
+            all_gain[shard] = own_gain[...]
+
+        @pl.when(jnp.logical_not(is_hub))
+        def _():
+            to_hub().start()
+
         for far in (0, 1, 2, 3):
             layer = near[far]
             for number in both:
@@ -379,12 +398,18 @@
                 side_turn(step - 1)
             if 2 <= step:
                 corner_turn(step - 2)
+            if step == 1:
+                share_gain()
         for place in range(chips):
             for far in (0, 1, 2, 3):
                 for number in both:
                     pair_copy(number, place, far, 1 - core).wait_recv()
-        close_gain(own_gain, all_gain, 0)
-        gain = jnp.sum(all_gain[...], axis=0)[:1]
+        for place in range(chips):
+            wait_gain(2 * place + 1 - core)
+        gain_blocks = jnp.sum(all_gain[...], axis=0)
+        gain = jnp.concatenate(
+            [gain_blocks[i : i + 1, :] for i in range(features // BLOCK)], axis=1
+        )
     else:
         w_up, w_down, acc_gain = own_up, own_down, grad_gain
         gain = own_gain[:1]
@@ -410,8 +435,8 @@
         )
 
     def layer_norm(m):
-        mask = embed[m]
-        scale = width_inv[m][:, :1]
+        mask = embed(m)
+        scale = width_inv(m)
         values = x_in[m].astype(F32) * mask
         center = jnp.sum(values, axis=-1, keepdims=True) * scale
         centered = (values - center) * mask
@@ -419,16 +444,16 @@
         inv_std = lax.rsqrt(variance + EPSILON)
         return centered * inv_std, inv_std
 
-    def forward(m, carry):
+    def forward(m):
         at = pl.ds(pl.multiple_of(m * rows, rows), rows)
 
         @pl.when(is_first)
         def _():
             if planes:
                 wait_tokens(0, m)
-                x_in[m] = (x_in[m].astype(F32) * embed[m]).astype(BF16)
+                x_in[m] = (x_in[m].astype(F32) * embed(m)).astype(BF16)
             else:
-                x_in[m] = (patches[m].astype(F32) * embed[m]).astype(BF16)
+                x_in[m] = (patches[m].astype(F32) * embed(m)).astype(BF16)
 
         @pl.when(jnp.logical_not(is_first))
         def _():
@@ -437,12 +462,11 @@
         standard, _ = layer_norm(m)
         scaled = standard * gain
         normed = scaled.astype(BF16)
-        normed_t[:, at] = jnp.transpose(scaled).astype(BF16)
         for start, size in chunks(hidden_count, 512):
             part = pl.ds(start, size)
             hidden = jnp.dot(normed, w_up[:, part], preferred_element_type=F32)
             value, rise = gelu_and_slope(hidden)
-            mask = hidden_mask[m, :, part]
+            mask = hidden_mask(m, part)
             act[at, part] = (value * mask).astype(BF16)
             slope[at, part] = (rise * mask).astype(BF16)
 
@@ -451,34 +475,41 @@
             for start, size in chunks(features, 256):
                 part = pl.ds(start, size)
                 branch = jnp.dot(act[at, :], w_down[:, part], preferred_element_type=F32)
-                out = x_in[m, :, part].astype(F32) + live[m, :, part] * branch
+                out = x_in[m, :, part].astype(F32) + live(m, part) * branch
                 x_out[m, :, part] = out.astype(BF16)
             forward_copy(m).start()
 
+        return scaled
+
+    def whole_micro(number):
+        return pl.ds(pl.multiple_of(number * halves * rows, halves * rows), halves * rows)
+
+    def forward_micro(number, carry):
+        parts = [forward(number * halves + half) for half in range(halves)]
+        normed_t[:, whole_micro(number)] = jnp.transpose(jnp.concatenate(parts, axis=0)).astype(BF16)
         return carry
 
-    lax.fori_loop(0, micro_count, forward, 0)
+    lax.fori_loop(0, micro_count // halves, forward_micro, 0)
     acc_gain[...] = jnp.zeros_like(acc_gain)
 
-    def backward(m, carry):
+    def backward(m):
         at = pl.ds(pl.multiple_of(m * rows, rows), rows)
 
         @pl.when(is_last)
         def _():
             if planes:
                 wait_tokens(1, m)
-                g_in[m] = (g_in[m].astype(F32) * embed[m]).astype(BF16)
+                g_in[m] = (g_in[m].astype(F32) * embed(m)).astype(BF16)
             else:
-                g_in[m] = (cotangent[m].astype(F32) * embed[m]).astype(BF16)
+                g_in[m] = (cotangent[m].astype(F32) * embed(m)).astype(BF16)
 
         @pl.when(jnp.logical_not(is_last))
         def _():
             backward_copy(m).wait_recv()
 
         grad_float = g_in[m].astype(F32)
-        branch_float = grad_float * live[m]
+        branch_float = grad_float * live(m)
         branch = branch_float.astype(BF16)
-        branch_t[:, at] = jnp.transpose(branch_float).astype(BF16)
         for start, size in chunks(hidden_count, 512):
             part = pl.ds(start, size)
             grad_act = contract_last(branch, w_down[part, :])
@@ -492,8 +523,8 @@
             axis=1,
         )
         standard, inv_std = layer_norm(m)
-        mask = embed[m]
-        scale = width_inv[m][:, :1]
+        mask = embed(m)
+        scale = width_inv(m)
         acc_gain[...] += jnp.sum((grad_normed * standard).reshape(-1, 8, features), axis=0)
 
         @pl.when(jnp.logical_not(is_first))
@@ -505,9 +536,14 @@
             g_out[m] = (grad_float + grad_x).astype(BF16)
             backward_copy(m).start()
 
+        return branch_float
+
+    def backward_micro(number, carry):
+        parts = [backward(number * halves + half) for half in range(halves)]
+        branch_t[:, whole_micro(number)] = jnp.transpose(jnp.concatenate(parts, axis=0)).astype(BF16)
         return carry
 
-    lax.fori_loop(0, micro_count, backward, 0)
+    lax.fori_loop(0, micro_count // halves, backward_micro, 0)
 
     width = 256 if hidden_count % 256 == 0 else hidden_count
 
@@ -654,13 +690,57 @@
             def _():
                 second_turn(place_at(jnp.maximum(index - 1, 0)))
 
+            @pl.when(jnp.logical_and(index == chips, is_hub))
+            def _():
+                hub_turn()
+
             @pl.when(index >= 2)
             def _():
                 plane_turn(place_at(jnp.maximum(index - 2, 0)))
 
             return carry
 
-        open_gain(acc_gain, all_rise, 1)
+        rise = jnp.sum(acc_gain[...], axis=0, keepdims=True)
+        spare = own_gain.shape[0] - features // BLOCK
+        rise_rows = [rise[:, i : i + BLOCK] for i in range(0, features, BLOCK)]
+        if spare:
+            rise_rows.append(jnp.zeros((spare, BLOCK), F32))
+        rise_own[...] = jnp.concatenate(rise_rows, axis=0)
+
+        def rise_copy(source, target, way, device):
+            return remote(source, all_rise.at[target], rise_send.at[way], rise_recv.at[target], device)
+
+        def rise_to_hub():
+            return rise_copy(rise_own, column, 0, {"section": chip})
+
+        def rise_to_pair():
+            return rise_copy(rise_own, chips, 1, other)
+
+        def rise_to_place(place):
+            return rise_copy(rise_sum, chips + 1, 2 + place, {"fsdp": 2 * place + core})
+
+        def rise_wait(target):
+            rise_copy(all_rise.at[target], target, 0, other).wait_recv()
+
+        @pl.when(jnp.logical_not(is_hub))
+        def _():
+            rise_to_hub().start()
+
+        def hub_turn():
+            total = rise_own[...]
+            for far in (1, 2, 3):
+                rise_wait(near[far])
+                total = total + all_rise[near[far]]
+            rise_own[...] = total
+            rise_to_pair().start()
+            rise_wait(chips)
+            rise_sum[...] = total + all_rise[chips]
+            for place in range(chips):
+
+                @pl.when(place != chip)
+                def _():
+                    rise_to_place(place).start()
+
         for number in both:
             for far in (1, 2, 3):
                 scatter_copy(number, far).wait_send()
@@ -676,7 +756,19 @@
                 relay(number, place).wait_send()
                 for far in (0, 1, 2, 3):
                     pair_copy(number, place, far, core).wait_send()
-        sent_gain(own_gain, all_gain, 0)
+
+        @pl.when(is_hub)
+        def _():
+            for place in range(chips):
+                for far in (0, 1, 2, 3):
+                    from_hub(place, far).wait_send()
+
+        @pl.when(jnp.logical_not(is_hub))
+        def _():
+            to_hub().wait_send()
+            for place in range(chips):
+                from_hub(place, 0).wait_send()
+
         lax.fori_loop(0, chips + 2, reduce_step, 0)
         for layer in reversed(range(chips)):
             for number in both:
@@ -693,8 +785,22 @@
                 def _():
                     lasts[number][layer] = finals[number][layer]
 
-        close_gain(acc_gain, all_rise, 1)
-        grad_gain[...] = jnp.sum(all_rise[...], axis=0)
+        @pl.when(is_hub)
+        def _():
+            grad_gain[...] = rise_sum[...]
+            rise_to_pair().wait_send()
+            for place in range(chips):
+
+                @pl.when(place != chip)
+                def _():
+                    rise_to_place(place).wait_send()
+
+        @pl.when(jnp.logical_not(is_hub))
+        def _():
+            rise_wait(chips + 1)
+            grad_gain[...] = all_rise[chips + 1]
+            rise_to_hub().wait_send()
+
         for source in range(section_count):
             for number in both:
 
@@ -704,7 +810,6 @@
 
             grad_up[:, pl.ds(source * up_cols, up_cols)] = last_up[source].astype(F32)
             grad_down[pl.ds(source * down_part, down_part), :] = last_down[source].astype(F32)
-        sent_gain(acc_gain, all_rise, 1)
         for number in both:
             for place in range(chips):
                 sum_pair(number, place).wait_send()
@@ -743,7 +848,7 @@
     lax.fori_loop(0, micro_count, drain, 0)
 
 
-def run_pipeline(planes, patches, cotangent, embed, live, hidden_mask, width_inv, gain, w_up, w_down):
+def run_pipeline(planes, patches, cotangent, table, gain, w_up, w_down):
     section_count = lax.axis_size("section")
     shard_count = lax.axis_size("fsdp")
     micro_count, rows, features = patches.shape
@@ -776,8 +881,10 @@
             pltpu.VMEM((hidden_count, features), BF16),
             pltpu.VMEM((section_count,) + up_piece, BF16),
             pltpu.VMEM((section_count,) + down_piece, BF16),
-            pltpu.VMEM((shard_count, 8, features), F32),
-            pltpu.VMEM((shard_count, 8, features), F32),
+            pltpu.VMEM((shard_count,) + gain.shape, F32),
+            pltpu.VMEM((chips + 2,) + gain.shape, F32),
+            pltpu.VMEM(gain.shape, F32),
+            pltpu.VMEM(gain.shape, F32),
             pltpu.VMEM((8, features), F32),
             pltpu.VMEM((chips, up_rows, hidden_count), BF16),
             pltpu.VMEM((chips, down_rows, features), BF16),
@@ -791,8 +898,10 @@
             pltpu.VMEM((section_count,) + down_piece, BF16),
             dma((2, micro_count)),
             dma((2, micro_count, chips)),
-            dma((2, shard_count)),
-            dma((2, shard_count)),
+            dma((5, chips)),
+            dma((shard_count,)),
+            dma((2 + chips,)),
+            dma((2 + chips,)),
             dma((2, 3)),
             dma((2, section_count)),
             dma((2, chips)),
@@ -823,14 +932,14 @@
         )
     return pl.pallas_call(
         functools.partial(pipeline_kernel, section_count, shard_count),
-        out_shape=grads + (jax.ShapeDtypeStruct((8, features), F32),),
-        in_specs=[vmem] * 9,
+        out_shape=grads + (jax.ShapeDtypeStruct(gain.shape, F32),),
+        in_specs=[vmem] * 6,
         out_specs=(vmem, vmem, vmem),
         scratch_shapes=scratch,
         compiler_params=pltpu.CompilerParams(
             collective_id=0, has_side_effects=True, vmem_limit_bytes=VMEM_BYTES
         ),
-    )(patches, cotangent, embed, live, hidden_mask, width_inv, gain, w_up, w_down)
+    )(patches, cotangent, table, gain, w_up, w_down)
 
 
 def per_device(patches, cotangent, embed_blocks, ratio_index, depth, w_up, w_down, ln_gain):
@@ -853,22 +962,28 @@
 
     width = embed_blocks * BLOCK
     hidden_width = width * (6 + ratio_index) // 2
-    embed = (lax.iota(jnp.int32, features)[None, :] < width[:, None]).astype(F32)
-    hidden_mask = (lax.iota(jnp.int32, hidden_count)[None, :] < hidden_width[:, None]).astype(F32)
     layer = shard_index // 2 if planes else section_index
-    active = (layer < depth).astype(F32)
-    live = embed * active[:, None]
-    width_inv = jnp.broadcast_to((1.0 / width.astype(F32))[:, None, None], (micro_count, 1, BLOCK))
-    masks = (embed[:, None, :], live[:, None, :], hidden_mask[:, None, :], width_inv)
+    active = (layer < depth).astype(F32)[:, None, None]
+    row = lax.broadcasted_iota(jnp.int32, (micro_count, 8, hidden_count), 1)
+    unit = lax.broadcasted_iota(jnp.int32, (micro_count, 8, hidden_count), 2)
+    limit = jnp.where(row == 0, hidden_width[:, None, None], width[:, None, None])
+    value = jnp.where(row == 2, active, 1.0)
+    table = jnp.where(unit < limit, value, 0.0)
+    table = jnp.where(row == 3, 1.0 / width.astype(F32)[:, None, None], table)
     start = shard_index * gain_count
 
     if planes:
-        gain = jnp.zeros((8, features), F32)
-        gain = lax.dynamic_update_slice(gain, ln_gain.astype(F32), (jnp.int32(0), start))
+        halves = 2 if rows % (32 * section_count) == 0 and SPLIT else 1
+        gain_rows = -(-features // (8 * BLOCK)) * 8
+        spot = lax.iota(jnp.int32, gain_rows * BLOCK)
+        repeats = -(-gain_rows * BLOCK // gain_count)
+        gain = jnp.tile(ln_gain[0].astype(F32), repeats)[: gain_rows * BLOCK]
+        gain = jnp.where(spot // gain_count == shard_index, gain, 0.0).reshape(gain_rows, BLOCK)
+        split = (micro_count * halves, rows // halves, features)
         own_up, own_down, gains = run_pipeline(
-            True, patches, cotangent, *masks, gain, w_up[0], w_down[0]
+            True, patches.reshape(split), cotangent.reshape(split), table, gain, w_up[0], w_down[0]
         )
-        own_gain = lax.dynamic_slice(jnp.sum(gains, axis=0), (start,), (gain_count,))
+        own_gain = lax.dynamic_slice(gains.reshape(-1), (start,), (gain_count,))
         return (own_up[None], own_down[None], own_gain[None])
 
     full_up = lax.all_gather(w_up[0], "fsdp", axis=0, tiled=True)
@@ -876,7 +991,7 @@
     gain = lax.all_gather(ln_gain[0], "fsdp", axis=0, tiled=True).astype(F32)
     gain = jnp.broadcast_to(gain[None], (8, features))
     part_up, part_down, gains = run_pipeline(
-        False, patches, cotangent, *masks, gain, full_up, full_down
+        False, patches, cotangent, table, gain, full_up, full_down
     )
     own_down = lax.psum_scatter(part_down, "fsdp", scatter_dimension=0, tiled=True)
     own_up = lax.psum_scatter(part_up, "fsdp", scatter_dimension=0, tiled=True)

time: 286 us -> 270 us (0.944)
  Pallas kernels: 273 us -> 259 us
    pallas_call x1, Pallas kernels: 273 us -> 259 us  [run_pipeline(): pl.pallas_call(functools.partial(pipeline_kernel, section_count, shard_co...]
where the time goes in v4:
time: 270 us; the launch traced here: 269 us
  Pallas kernels  259 us (96%)
  local copies, waits for them, and re-layouts  4.82 us (2%)
  other arithmetic  4.37 us (2%)
    pallas_call x1, Pallas kernels, run_pipeline(): pl.pallas_call(functools.partial(pipeline_kernel, section_count, shard_co...  259 us

profile of v4, /device:TPU:0, one launch (start us, length us, event | category | flops | bytes accessed | tf_op | source)
XLA Modules:
  0.0 268.6 jit_solution(1036894056505184924)
XLA Ops:
  0.6 0.7 bitcast_convert_fusion
  1.3 0.7 convert_divide_fusion
  2.0 0.7 compare_convert_fusion
  2.6 0.7 and_select_fusion
  3.3 0.1 tile.17
  3.4 0.6 fusion.1.own_gain
  4.0 1.1 select_select_fusion.table
  5.1 258.8 %shard_map.103 = (f32[96,3072]{1,0:T(8,128)}, f32[384,768]{1,0:T(8,128)}, f32[8,128]{1,0:T(8,128)}) custom-call(bf16[8,128,768]{2,1,0:T(8,128)(2,1)} %patches.1, bf16[8,128,768]{2,1,0:T(8,128)(2,1)} %cotangent.1, f32[8,8,3072]{2,1,0:T(8,128)} %select_select_fusion.table, f32[8,128]{1,0:T(8,128)} %fusion.1.own_gain, bf16[96,3072]{1,0:T(8,128)(2,1)} %bitcast.16, ...), custom_call_target="tpu_custom_call" | custom-call | tf_op jit(solution)/shard_map/pallas_call | solution.py:933
  263.9 1.3 dynamic-slice_bitcast_fusion
  265.2 0.0 copy-start
  265.2 2.5 copy.13
  267.6 0.0 copy-done
  267.6 1.0 copy.14
  (2 shorter events, 0.0 us)
Async XLA Ops:
  265.2 2.5 copy-start

commit v5 on v4

--- a/solution.py
+++ b/solution.py
@@ -10,6 +10,7 @@
 
 BLOCK = 128
 SPLIT = False
+LAG = 4
 EPSILON = 1e-05
 SCALE = 0.7978845608028654
 MESH = pl.DeviceIdType.MESH
@@ -359,9 +360,6 @@
                     spot = piece(number, fulls[number], chip, column)
                     spot[...] = source[...]
 
-        send_tokens(0, 1, micro_count)
-        send_tokens(1, 0, micro_count)
-
         def own_turn(step):
             place = lax.rem(chip + step, chips)
             for number in both:
@@ -394,6 +392,9 @@
         for step in range(chips + 2):
             if step < chips:
                 own_turn(step)
+            if step == chips - 1:
+                send_tokens(0, 1, micro_count)
+                send_tokens(1, 0, micro_count)
             if 1 <= step <= chips:
                 side_turn(step - 1)
             if 2 <= step:
@@ -489,7 +490,6 @@
         normed_t[:, whole_micro(number)] = jnp.transpose(jnp.concatenate(parts, axis=0)).astype(BF16)
         return carry
 
-    lax.fori_loop(0, micro_count // halves, forward_micro, 0)
     acc_gain[...] = jnp.zeros_like(acc_gain)
 
     def backward(m):
@@ -543,7 +543,23 @@
         branch_t[:, whole_micro(number)] = jnp.transpose(jnp.concatenate(parts, axis=0)).astype(BF16)
         return carry
 
-    lax.fori_loop(0, micro_count // halves, backward_micro, 0)
+    micro_total = micro_count // halves
+    lag = jnp.minimum(LAG * (stages - 1 - me), micro_total)
+
+    def turn(number, carry):
+        @pl.when(number < micro_total)
+        def _():
+            forward_micro(jnp.minimum(number, micro_total - 1), 0)
+
+        late = number - lag
+
+        @pl.when(jnp.logical_and(late >= 0, late < micro_total))
+        def _():
+            backward_micro(jnp.clip(late, 0, micro_total - 1), 0)
+
+        return carry
+
+    lax.fori_loop(0, 2 * micro_total, turn, 0)
 
     width = 256 if hidden_count % 256 == 0 else hidden_count
 

time: 270 us -> 248 us (0.919)
  Pallas kernels: 259 us -> 237 us
    pallas_call x1, Pallas kernels: 259 us -> 237 us  [run_pipeline(): pl.pallas_call(functools.partial(pipeline_kernel, section_count, shard_co...]
where the time goes in v5:
time: 248 us; the launch traced here: 247 us
  Pallas kernels  237 us (96%)
  local copies, waits for them, and re-layouts  4.82 us (2%)
  other arithmetic  4.37 us (2%)
    pallas_call x1, Pallas kernels, run_pipeline(): pl.pallas_call(functools.partial(pipeline_kernel, section_count, shard_co...  237 us

profile of v5, /device:TPU:0, one launch (start us, length us, event | category | flops | bytes accessed | tf_op | source)
XLA Modules:
  0.0 247.0 jit_solution(13289242392436645538)
XLA Ops:
  0.6 0.7 bitcast_convert_fusion
  1.3 0.7 convert_divide_fusion
  2.0 0.7 compare_convert_fusion
  2.6 0.7 and_select_fusion
  3.3 0.1 tile.17
  3.4 0.6 fusion.1.own_gain
  4.0 1.1 select_select_fusion.table
  5.1 237.2 %shard_map.103 = (f32[96,3072]{1,0:T(8,128)}, f32[384,768]{1,0:T(8,128)}, f32[8,128]{1,0:T(8,128)}) custom-call(bf16[8,128,768]{2,1,0:T(8,128)(2,1)} %patches.1, bf16[8,128,768]{2,1,0:T(8,128)(2,1)} %cotangent.1, f32[8,8,3072]{2,1,0:T(8,128)} %select_select_fusion.table, f32[8,128]{1,0:T(8,128)} %fusion.1.own_gain, bf16[96,3072]{1,0:T(8,128)(2,1)} %bitcast.16, ...), custom_call_target="tpu_custom_call" | custom-call | tf_op jit(solution)/shard_map/pallas_call | solution.py:949
  242.3 1.3 dynamic-slice_bitcast_fusion
  243.5 0.0 copy-start
  243.5 2.5 copy.13
  246.0 0.0 copy-done
  246.0 1.0 copy.14
  (2 shorter events, 0.0 us)
Async XLA Ops:
  243.5 2.5 copy-start

commit v6 on v5

--- a/solution.py
+++ b/solution.py
@@ -45,7 +45,9 @@
     shard_count,
     patches,
     cotangent,
-    table,
+    embed_blocks,
+    ratio_index,
+    depth,
     own_gain,
     own_up,
     own_down,
@@ -60,6 +62,7 @@
     slope,
     normed_t,
     branch_t,
+    table,
     fwd_send,
     fwd_recv,
     bwd_send,
@@ -119,9 +122,22 @@
     is_first = me == 0
     is_last = me == stages - 1
     micro_count, rows, features = patches.shape
-    hidden_count = table.shape[2]
+    hidden_count = own_up.shape[1]
     features_all = pl.ds(0, features)
     halves = micro_count // table.shape[0]
+
+    def build_table():
+        for m in range(table.shape[0]):
+            unit = lax.broadcasted_iota(jnp.int32, (1, hidden_count), 1)
+            blocks = embed_blocks[m]
+            hidden_width = blocks * (BLOCK // 2) * (6 + ratio_index[m])
+            mask = jnp.where(unit < blocks * BLOCK, 1.0, 0.0)
+            active = jnp.where(me < depth[m], 1.0, 0.0)
+            width = jnp.full((1, BLOCK), blocks * BLOCK, jnp.int32).astype(F32)
+            table[m, 0:1, :] = jnp.where(unit < hidden_width, 1.0, 0.0)
+            table[m, 1:2, :] = mask
+            table[m, 2:3, :] = mask * active
+            table[m, 3:4, 0:BLOCK] = 1.0 / width
 
     def hidden_mask(m, part):
         return table[m // halves, 0:1, part]
@@ -342,6 +358,7 @@
         def _():
             to_hub().start()
 
+        build_table()
         for far in (0, 1, 2, 3):
             layer = near[far]
             for number in both:
@@ -412,15 +429,19 @@
             [gain_blocks[i : i + 1, :] for i in range(features // BLOCK)], axis=1
         )
     else:
+        build_table()
         w_up, w_down, acc_gain = own_up, own_down, grad_gain
         gain = own_gain[:1]
 
-    def forward_copy(m):
+    columns = chunks(features, 256)
+
+    def forward_copy(m, index):
+        start, size = columns[index]
         return pltpu.make_async_remote_copy(
-            src_ref=x_out.at[m],
-            dst_ref=x_in.at[m],
-            send_sem=fwd_send.at[m],
-            recv_sem=fwd_recv.at[m],
+            src_ref=x_out.at[m, :, pl.ds(start, size)],
+            dst_ref=x_in.at[m, :, pl.ds(start, size)],
+            send_sem=fwd_send.at[m, index],
+            recv_sem=fwd_recv.at[m, index],
             device_id=stage_device(jnp.minimum(me + 1, stages - 1)),
             device_id_type=MESH,
         )
@@ -458,7 +479,8 @@
 
         @pl.when(jnp.logical_not(is_first))
         def _():
-            forward_copy(m).wait_recv()
+            for index in range(len(columns)):
+                forward_copy(m, index).wait_recv()
 
         standard, _ = layer_norm(m)
         scaled = standard * gain
@@ -473,12 +495,12 @@
 
         @pl.when(jnp.logical_not(is_last))
         def _():
-            for start, size in chunks(features, 256):
+            for index, (start, size) in enumerate(columns):
                 part = pl.ds(start, size)
                 branch = jnp.dot(act[at, :], w_down[:, part], preferred_element_type=F32)
                 out = x_in[m, :, part].astype(F32) + live(m, part) * branch
                 x_out[m, :, part] = out.astype(BF16)
-            forward_copy(m).start()
+                forward_copy(m, index).start()
 
         return scaled
 
@@ -824,8 +846,8 @@
                 def _():
                     last_copy(number, source, source).wait_recv()
 
-            grad_up[:, pl.ds(source * up_cols, up_cols)] = last_up[source].astype(F32)
-            grad_down[pl.ds(source * down_part, down_part), :] = last_down[source].astype(F32)
+            grad_up[:, pl.ds(source * up_cols, up_cols)] = last_up[source]
+            grad_down[pl.ds(source * down_part, down_part), :] = last_down[source]
         for number in both:
             for place in range(chips):
                 sum_pair(number, place).wait_send()
@@ -853,7 +875,8 @@
     def drain(m, carry):
         @pl.when(jnp.logical_not(is_last))
         def _():
-            forward_copy(m).wait_send()
+            for index in range(len(columns)):
+                forward_copy(m, index).wait_send()
 
         @pl.when(jnp.logical_not(is_first))
         def _():
@@ -864,7 +887,7 @@
     lax.fori_loop(0, micro_count, drain, 0)
 
 
-def run_pipeline(planes, patches, cotangent, table, gain, w_up, w_down):
+def run_pipeline(planes, patches, cotangent, scalars, gain, w_up, w_down):
     section_count = lax.axis_size("section")
     shard_count = lax.axis_size("fsdp")
     micro_count, rows, features = patches.shape
@@ -883,8 +906,9 @@
         pltpu.VMEM((tokens, hidden_count), BF16),
         pltpu.VMEM((features, tokens), BF16),
         pltpu.VMEM((features, tokens), BF16),
-        dma((micro_count,)),
-        dma((micro_count,)),
+        pltpu.VMEM(scalars[0].shape + (8, hidden_count), F32),
+        dma((micro_count, len(chunks(features, 256)))),
+        dma((micro_count, len(chunks(features, 256)))),
         dma((micro_count,)),
         dma((micro_count,)),
     ]
@@ -938,8 +962,8 @@
             dma((2, section_count)),
         ]
         grads = (
-            jax.ShapeDtypeStruct((up_rows, hidden_count), F32),
-            jax.ShapeDtypeStruct((down_rows, features), F32),
+            jax.ShapeDtypeStruct((up_rows, hidden_count), BF16),
+            jax.ShapeDtypeStruct((down_rows, features), BF16),
         )
     else:
         grads = (
@@ -949,17 +973,16 @@
     return pl.pallas_call(
         functools.partial(pipeline_kernel, section_count, shard_count),
         out_shape=grads + (jax.ShapeDtypeStruct(gain.shape, F32),),
-        in_specs=[vmem] * 6,
+        in_specs=[vmem] * 2 + [pl.BlockSpec(memory_space=pltpu.SMEM)] * 3 + [vmem] * 3,
         out_specs=(vmem, vmem, vmem),
         scratch_shapes=scratch,
         compiler_params=pltpu.CompilerParams(
             collective_id=0, has_side_effects=True, vmem_limit_bytes=VMEM_BYTES
         ),
-    )(patches, cotangent, table, gain, w_up, w_down)
+    )(patches, cotangent, *scalars, gain, w_up, w_down)
 
 
 def per_device(patches, cotangent, embed_blocks, ratio_index, depth, w_up, w_down, ln_gain):
-    section_index = lax.axis_index("section")
     shard_index = lax.axis_index("fsdp")
     shard_count = lax.axis_size("fsdp")
     micro_count, rows, features = patches.shape
@@ -976,16 +999,7 @@
         and rows % (16 * section_count) == 0
     )
 
-    width = embed_blocks * BLOCK
-    hidden_width = width * (6 + ratio_index) // 2
-    layer = shard_index // 2 if planes else section_index
-    active = (layer < depth).astype(F32)[:, None, None]
-    row = lax.broadcasted_iota(jnp.int32, (micro_count, 8, hidden_count), 1)
-    unit = lax.broadcasted_iota(jnp.int32, (micro_count, 8, hidden_count), 2)
-    limit = jnp.where(row == 0, hidden_width[:, None, None], width[:, None, None])
-    value = jnp.where(row == 2, active, 1.0)
-    table = jnp.where(unit < limit, value, 0.0)
-    table = jnp.where(row == 3, 1.0 / width.astype(F32)[:, None, None], table)
+    scalars = (embed_blocks, ratio_index, depth)
     start = shard_index * gain_count
 
     if planes:
@@ -997,17 +1011,17 @@
         gain = jnp.where(spot // gain_count == shard_index, gain, 0.0).reshape(gain_rows, BLOCK)
         split = (micro_count * halves, rows // halves, features)
         own_up, own_down, gains = run_pipeline(
-            True, patches.reshape(split), cotangent.reshape(split), table, gain, w_up[0], w_down[0]
+            True, patches.reshape(split), cotangent.reshape(split), scalars, gain, w_up[0], w_down[0]
         )
         own_gain = lax.dynamic_slice(gains.reshape(-1), (start,), (gain_count,))
-        return (own_up[None], own_down[None], own_gain[None])
+        return (own_up.astype(F32)[None], own_down.astype(F32)[None], own_gain[None])
 
     full_up = lax.all_gather(w_up[0], "fsdp", axis=0, tiled=True)
     full_down = lax.all_gather(w_down[0], "fsdp", axis=0, tiled=True)
     gain = lax.all_gather(ln_gain[0], "fsdp", axis=0, tiled=True).astype(F32)
     gain = jnp.broadcast_to(gain[None], (8, features))
     part_up, part_down, gains = run_pipeline(
-        False, patches, cotangent, table, gain, full_up, full_down
+        False, patches, cotangent, scalars, gain, full_up, full_down
     )
     own_down = lax.psum_scatter(part_down, "fsdp", scatter_dimension=0, tiled=True)
     own_up = lax.psum_scatter(part_up, "fsdp", scatter_dimension=0, tiled=True)

time: 248 us -> 245 us (0.988)
  local copies, waits for them, and re-layouts: 4.82 us -> 1.4 us
    unnamed x4 -> x2, local copies, waits for them, and re-layouts: 3.47 us -> 0.01 us
    broadcast_in_dim x0 -> x2, other arithmetic: none -> 3.27 us  [the longest x1 2.18 us: per_device(): own_up.astype(F32)[None]]
where the time goes in v6:
time: 245 us; the launch traced here: 244 us
  Pallas kernels  238 us (97%)
  other arithmetic  4.54 us (2%)
    pallas_call x1, Pallas kernels, run_pipeline(): pl.pallas_call(functools.partial(pipeline_kernel, section_count, shard_co...  238 us

profile of v6, /device:TPU:0, one launch (start us, length us, event | category | flops | bytes accessed | tf_op | source)
XLA Modules:
  0.0 244.4 jit_solution(2676824396639269567)
XLA Ops:
  0.6 0.7 bitcast_convert_fusion.2
  1.3 0.1 tile.17
  1.4 0.6 fusion.1.own_gain
  2.0 237.8 %shard_map.103 = (bf16[96,3072]{1,0:T(8,128)(2,1)}, bf16[384,768]{1,0:T(8,128)(2,1)}, f32[8,128]{1,0:T(8,128)}) custom-call(bf16[8,128,768]{2,1,0:T(8,128)(2,1)} %patches.1, bf16[8,128,768]{2,1,0:T(8,128)(2,1)} %cotangent.1, s32[8]{0:T(128)} %embed_blocks.1, s32[8]{0:T(128)} %ratio_index.1, s32[8]{0:T(128)} %depth.1, f32[8,128]{1,0:T(8,128)} %fusion.1.own_gain, ...), custom_call_target="tpu_custom_call" | custom-call | tf_op jit(solution)/shard_map/pallas_call | solution.py:973
  239.8 0.0 copy-start
  239.8 1.3 dynamic-slice_bitcast_fusion
  241.1 2.2 bitcast_convert_fusion.1
  243.3 0.0 copy-done
  243.3 1.1 bitcast_convert_fusion
  (1 shorter events, 0.0 us)
Async XLA Ops:
  239.8 3.5 %copy-start = (bf16[384,768]{1,0:T(8,128)(2,1)S(1)}, bf16[384,768]{1,0:T(8,128)(2,1)}, u32[]{:S(2)}) copy-start(bf16[384,768]{1,0:T(8,128)(2,1)} %get-tuple-element.7) | copy-start | bytes 1769476
